TPU v7x, 768 devices: a whole 4x8x12 slice. The times are simulated.
768 devices in a mesh: blk: 96 (over y, z_lo, x), grp: 8 (over z_hi, core).
Axes of the slice: x: 4, y: 8, z: 12 (z_hi: 4, z_lo: 3; z = z_hi * 3 + z_lo), core: 2. Of those that a mesh axis runs over, the one named last changes fastest.
Arguments:
- tokens: bfloat16 [98304, 4096], P(('blk', 'grp')), may hold values from -6 to 6
- select: int32 [8, 192], P('grp', 'blk'), may hold values from 0 to 98303, as said below
- gates: float32 [8, 192], P('grp', 'blk'), may hold values from 0.1 to 1
- gate_proj: bfloat16 [8, 10752, 4096], P('grp', 'blk'), may hold values from -0.09375 to 0.09375
- up_proj: bfloat16 [8, 10752, 4096], P('grp', 'blk'), may hold values from -0.09375 to 0.09375
- down_proj: bfloat16 [8, 10752, 4096], P('grp', 'blk'), may hold values from -0.0625 to 0.0625
Outputs:
- mixed: bfloat16 [98304, 4096], P(('blk', 'grp'))
Inputs may be any that keep to these rules, and one draw needn't show every extreme that they name: `select`: for every expert and every k, the slots k * 2 to (k + 1) * 2 - 1 name 2 different tokens, all from k * 8 * 128 to (k + 1) * 8 * 128 - 1.
All inputs are finite; a program needn't handle non-finite values.
Results may differ from a plain program's by a relative error of at most 0.0095.
Values may be sent and summed in bfloat16 or wider, within the bound.
A program may use at most 32 MiB of HBM per device.

v0:
```python
import jax
import jax.numpy as jnp
from jax import lax
from jax.sharding import Mesh
from jax.sharding import PartitionSpec as P

BLK = ("blk_0", "blk_1", "blk_2")
BLK_GRP = ("blk_0", "blk_1", "blk_2", "grp")


def sent_to_all(array, axis):
    copies = jnp.broadcast_to(array, (lax.axis_size(axis), *array.shape))
    return lax.all_to_all(copies, axis, split_axis=0, concat_axis=0, tiled=True)


def laid_out(blocks, dim):
    dims = list(blocks.shape[1:])
    dims[dim] *= blocks.shape[0]
    return jnp.moveaxis(blocks, 0, dim).reshape(dims)


def collect(array, axis, dim):
    blocks = sent_to_all(array, axis)
    return laid_out(blocks, dim)


def all_blocks(array, axes, sequence):
    blocks = array
    for k in sequence:
        blocks = lax.all_gather(blocks, axes[k])
    done = sequence[::-1]
    back = [done.index(k) for k in range(len(axes))]
    blocks = blocks.transpose(*back, *range(len(axes), blocks.ndim))
    return blocks.reshape(-1, *array.shape)


def whole_of(array, axes, sequence, dim):
    return laid_out(all_blocks(array, axes, sequence), dim)


def cut_along(array, dim, size):
    before, after = (array.shape[:dim], array.shape[dim + 1 :])
    return jnp.moveaxis(array.reshape(*before, size, -1, *after), dim, 0)


def sum_in_tiles(array, axis, dim):
    size = lax.axis_size(axis)
    blocks = cut_along(array, dim, size)
    length = array.size // size
    spare = max(2048 - length, -length % 1024)
    padded = jnp.pad(blocks.reshape(size, length), ((0, 0), (0, spare)))
    own = lax.psum_scatter(padded.reshape(-1, 128), axis, scatter_dimension=0, tiled=True)
    return own.reshape(-1)[:length].reshape(blocks.shape[1:])


def on_device(tokens, select, gates, gate_proj, up_proj, down_proj):
    groups = lax.axis_size("grp")
    tok_dev = tokens.shape[0]
    width = tokens.shape[1]
    slots = select.shape[1]
    first = (lax.axis_index(BLK) * groups + lax.axis_index("grp")) * tok_dev
    all_ids = collect(select, "grp", 0)
    local_ids = all_ids.reshape(-1) - first
    owned = (local_ids[:, None] == jnp.arange(tok_dev, dtype=jnp.int32)[None, :]).astype(
        jnp.bfloat16
    )
    candidates = jnp.dot(owned, tokens, preferred_element_type=jnp.float32)
    arrived = lax.all_to_all(
        candidates.astype(jnp.bfloat16), "grp", split_axis=0, concat_axis=0, tiled=True
    )
    picked = jnp.sum(arrived.reshape(groups, slots, width).astype(jnp.float32), axis=0).astype(
        jnp.bfloat16
    )
    w_gate = gate_proj[0]
    w_up = up_proj[0]
    w_down = down_proj[0]
    dims = (((1,), (1,)), ((), ()))
    piece = whole_of(picked, BLK, (1, 0, 2), 0)
    gate_act = lax.dot_general(piece, w_gate, dims, preferred_element_type=jnp.float32)
    up_act = lax.dot_general(piece, w_up, dims, preferred_element_type=jnp.float32)
    hidden = (jax.nn.silu(gate_act) * up_act).astype(jnp.bfloat16)
    summed = sum_in_tiles(jnp.dot(hidden, w_down, preferred_element_type=jnp.float32), BLK, 0)
    expert_out = summed.astype(jnp.bfloat16)
    weighted = (gates[0][:, None] * expert_out.astype(jnp.float32)).astype(jnp.bfloat16)
    owner_mask = owned.T
    mixed = jnp.dot(owner_mask, collect(weighted, "grp", 0), preferred_element_type=jnp.float32)
    return mixed.astype(jnp.bfloat16)


def solution(mesh):
    finer = Mesh(
        mesh.devices.reshape(8, 3, 4, mesh.shape["grp"]), ("blk_0", "blk_1", "blk_2", "grp")
    )
    in_specs = (
        P(BLK_GRP, None),
        P("grp", BLK),
        P("grp", BLK),
        P("grp", BLK, None),
        P("grp", BLK, None),
        P("grp", BLK, None),
    )
    out_specs = P(BLK_GRP, None)
    return jax.shard_map(
        on_device, mesh=finer, in_specs=in_specs, out_specs=out_specs, check_vma=False
    )
```

profile of v0, /device:TPU:1, one launch (start us, length us, event | category | flops | bytes accessed | tf_op | source)
XLA Modules:
  0.0 746.7 jit_solution(18333399280497134239)
XLA Ops:
  6.5 1.3 broadcast_in_dim.8
  7.9 16.0 %all-to-all-start = ((s32[8,1,2]{2,1,0:T(1,128)}), s32[8,1,2]{2,1,0:T(1,128)S(1)}, u32[]{:S(2)}, u32[]{:S(2)}) async-start(s32[8,1,2]{2,1,0:T(1,128)} %broadcast_in_dim.8), calls=%async_computation | async-start | bytes 8192 | tf_op jit(solution)/shard_map/all_to_all | solution.py:13
  23.9 9.3 %all-to-all-done = s32[8,1,2]{2,1,0:T(1,128)S(1)} async-done(((s32[8,1,2]{2,1,0:T(1,128)}), s32[8,1,2]{2,1,0:T(1,128)S(1)}, u32[]{:S(2)}, u32[]{:S(2)}) %all-to-all-start) | async-done | bytes 96 | tf_op jit(solution)/shard_map/all_to_all | solution.py:13
  33.2 0.1 sub.15
  33.3 0.3 convolution_convert_fusion.1
  33.6 0.1 all_to_all.13
  33.7 13.5 %all_to_all.19 = bf16[8,2,4096]{2,1,0:T(2,128)(2,1)S(1)} all-to-all(bf16[8,2,4096]{2,1,0:T(2,128)(2,1)S(1)} %all_to_all.13), channel_id=1, replica_groups=mesh['blk_0'=8,'blk_1'=3,'blk_2'=4,'grp'=8] {'grp'}, dimensions={0} | all-to-all | bytes 262144 | tf_op jit(solution)/shard_map/all_to_all | solution.py:68
  47.2 0.1 reduce_sum.12
  47.3 8.5 %all-gather.3 = bf16[3,2,4096]{2,1,0:T(2,128)(2,1)S(1)} all-gather(bf16[1,2,4096]{2,1,0:T(2,128)(2,1)S(1)} %bitcast.25), channel_id=2, replica_groups=mesh['blk_0'=8,'blk_1'=3,'blk_2'=4,'grp'=8] {'blk_1'}, dimensions={0}, use_global_device_ids=true | all-gather | bytes 65536 | tf_op jit(solution)/shard_map/all_gather | solution.py:30
  55.8 22.6 %all-gather.1 = bf16[24,2,4096]{2,1,0:T(2,128)(2,1)} all-gather(bf16[3,2,4096]{2,1,0:T(2,128)(2,1)S(1)} %all-gather.3), channel_id=3, replica_groups=mesh['blk_0'=8,'blk_1'=3,'blk_2'=4,'grp'=8] {'blk_0'}, dimensions={0}, use_global_device_ids=true | all-gather | bytes 442368 | tf_op jit(solution)/shard_map/all_gather | solution.py:30
  78.5 38.0 %all-gather.6.cloned.1.call-done = bf16[32,3,2,4096]{3,2,1,0:T(2,128)(2,1)} async-done(((bf16[8,3,2,4096]{3,2,1,0:T(2,128)(2,1)}), bf16[32,3,2,4096]{3,2,1,0:T(2,128)(2,1)}) %all-gather.6.cloned.1.call-update) | async-done | bytes 1572880 | tf_op jit(solution)/shard_map/all_gather | solution.py:30
  116.5 2.3 copy.13
  118.8 2.8 copy.11
  121.6 2.5 reshape_reshape.2
  124.1 2.5 fusion.5
  126.6 4.7 fusion.1
  131.3 4.6 reshape.23
  135.9 447.0 %reduce-scatter.2.cloned.1.call-done = f32[64,128]{1,0:T(8,128)} async-done(((f32[6144,128]{1,0:T(8,128)}), f32[64,128]{1,0:T(8,128)}) %reduce-scatter.2.cloned.1.call-update) | async-done | bytes 32784 | tf_op jit(solution)/shard_map/reduce_scatter | solution.py:52
  582.9 0.8 convert_convert_fusion
  583.7 0.1 multiply_convert_fusion
  583.8 0.1 broadcast_in_dim.9
  583.9 154.4 %all_to_all.20 = bf16[8,2,4096]{2,1,0:T(2,128)(2,1)S(1)} all-to-all(bf16[8,2,4096]{2,1,0:T(2,128)(2,1)S(1)} %broadcast_in_dim.9), channel_id=1, replica_groups=mesh['blk_0'=8,'blk_1'=3,'blk_2'=4,'grp'=8] {'grp'}, dimensions={0} | all-to-all | bytes 262144 | tf_op jit(solution)/shard_map/all_to_all | solution.py:13
  738.3 0.1 reshape.24
  738.4 1.5 convolution_convert_fusion
  (12 shorter events, 0.1 us)
Async XLA Ops:
  6.5 26.8 %copy-start = (bf16[128,4096]{1,0:T(8,128)(2,1)S(1)}, bf16[128,4096]{1,0:T(8,128)(2,1)}, u32[]{:S(2)}) copy-start(bf16[128,4096]{1,0:T(8,128)(2,1)} %param.6) | copy-start | bytes 3145732
  7.9 25.3 %all-to-all-start = ((s32[8,1,2]{2,1,0:T(1,128)}), s32[8,1,2]{2,1,0:T(1,128)S(1)}, u32[]{:S(2)}, u32[]{:S(2)}) async-start(s32[8,1,2]{2,1,0:T(1,128)} %broadcast_in_dim.8), calls=%async_computation | async-start | bytes 8192 | tf_op jit(solution)/shard_map/all_to_all | solution.py:13
  23.9 92.6 %all-gather.6.cloned.1.call-start = ((), (), s32[]{:S(2)}) async-start(), calls=%async_computation.5 | async-start | bytes 1966080 | tf_op jit(solution)/shard_map/all_gather | solution.py:30
  78.5 504.5 %reduce-scatter.2.cloned.1.call-start = ((), (), s32[]{:S(2)}) async-start(), calls=%async_computation.4 | async-start | bytes 3178496 | tf_op jit(solution)/shard_map/reduce_scatter | solution.py:52
  124.1 2.5 copy-start.1
  135.9 447.8 %copy-start.2 = (f32[1,2]{1,0:T(1,128)S(1)}, f32[1,2]{1,0:T(1,128)}, u32[]{:S(2)}) copy-start(f32[1,2]{1,0:T(1,128)} %param.8) | copy-start | bytes 28
Sparse Core Ops, SparseCore 0:
  78.6 37.8 all-gather.5
  136.0 446.8 reduce-scatter.1
where the time goes:
time: 747 us
  waiting for transfers between devices  494 us (66%)
  blocking collectives  199 us (27%)
  starting transfers between devices  16 us (2%)
  local copies, waits for them, and re-layouts  13.9 us (2%)
  between operations  13.5 us (2%)
  matrix products  8.98 us (1%)
    reduce_scatter x1, waiting for transfers between devices, sum_in_tiles(): lax.psum_scatter(padded.reshape(-1, 128), axis, scatter_dimension=0, tile...  447 us
    all_to_all x1, blocking collectives, sent_to_all(): return lax.all_to_all(copies, axis, split_axis=0, concat_axis=0, tiled=True)  154 us
    all_gather x1, waiting for transfers between devices, all_blocks(): blocks = lax.all_gather(blocks, axes[k])  38 us
    all_gather x2, blocking collectives, all_blocks(): blocks = lax.all_gather(blocks, axes[k])  31.1 us
    all_to_all x1, starting transfers between devices, sent_to_all(): return lax.all_to_all(copies, axis, split_axis=0, concat_axis=0, tiled=True)  16 us
  transfers between devices with their start and end apart: 3, of which 3 were waited for; matrix products, arithmetic and copies ran while one was open for 0% of the time, Pallas kernels for 0%

commit v1 on v0

v1 whole, which is shorter than its diff:
```python
import functools

import jax
import jax.numpy as jnp
import numpy as np
from jax import lax
from jax.experimental import pallas as pl
from jax.experimental.pallas import tpu as pltpu
from jax.sharding import Mesh
from jax.sharding import PartitionSpec as P

BLK = ("y", "z", "x")
BLK_GRP = ("y", "z", "x", "grp")
NY, NZ, NX = 8, 3, 4
YC, XC = 3, 3
YR, XR = NX * NZ * 2 // YC, NY * NZ * 2 // XC


def remote(src, dst, send_sem, recv_sem, **where):
    return pltpu.make_async_remote_copy(
        src_ref=src,
        dst_ref=dst,
        send_sem=send_sem,
        recv_sem=recv_sem,
        device_id=where,
        device_id_type=pl.DeviceIdType.MESH,
    )


def turn(index, by, size):
    return lax.rem(index + by + size, size)


def experts_kernel(
    picked,
    w_gate_hbm,
    w_up_hbm,
    w_down_hbm,
    perm,
    perm_t,
    out,
    w_gate,
    w_up,
    w_down,
    z_rows,
    x_rows,
    y_rows,
    rows_f32,
    ring_y,
    ring_x,
    part_y,
    part_x,
    send_y,
    send_x,
    recv_y,
    recv_x,
    flat_f32,
    mid_x_f32,
    mid_x,
    mid_x_recv,
    mid_y_f32,
    mid_y,
    mid_y_recv,
    mid_z_f32,
    mid_z,
    mid_z_recv,
    w_sem,
    gz_send,
    gz_recv,
    gx_send,
    gx_recv,
    gy_send,
    gy_recv,
    gry_send,
    gry_recv,
    grx_send,
    grx_recv,
    sry_send,
    sry_recv,
    srx_send,
    srx_recv,
    sx_send,
    sx_recv,
    sy_send,
    sy_recv,
    sz_send,
    sz_recv,
):
    y, z, x = lax.axis_index("y"), lax.axis_index("z"), lax.axis_index("x")
    width = picked.shape[-1]
    half = width // 2
    quarter = half // 2
    f32, bf16 = jnp.float32, jnp.bfloat16
    sent = []

    weights = [
        pltpu.make_async_copy(src.at[0], dst, w_sem.at[k])
        for k, (src, dst) in enumerate(
            ((w_gate_hbm, w_gate), (w_up_hbm, w_up), (w_down_hbm, w_down))
        )
    ]
    for copy in weights:
        copy.start()

    barrier = pltpu.get_barrier_semaphore()
    for o in range(1, NZ):
        pl.semaphore_signal(barrier, device_id={"z": turn(z, o, NZ)})
    for o in range(1, NX):
        pl.semaphore_signal(barrier, device_id={"x": turn(x, o, NX)})
    for o in range(1, NY):
        pl.semaphore_signal(barrier, device_id={"y": turn(y, o, NY)})
    pl.semaphore_wait(barrier, NZ + NX + NY - 3)

    def go(copy):
        copy.start()
        sent.append(copy)

    for o in range(1, NZ):
        go(remote(picked.at[0], z_rows.at[z], gz_send.at[o - 1], gz_recv.at[o - 1], z=turn(z, o, NZ)))
    z_rows[z] = picked[0]
    for o in range(1, NZ):
        landed = z_rows.at[turn(z, -o, NZ)]
        remote(landed, landed, gz_send.at[o - 1], gz_recv.at[o - 1], z=turn(z, o, NZ)).wait_recv()

    for o in range(1, NX):
        go(
            remote(
                z_rows.at[:, :, :half],
                x_rows.at[x],
                gx_send.at[o - 1],
                gx_recv.at[o - 1],
                x=turn(x, o, NX),
            )
        )
    for o in range(1, NY):
        go(
            remote(
                z_rows.at[:, :, half:],
                y_rows.at[y],
                gy_send.at[o - 1],
                gy_recv.at[o - 1],
                y=turn(y, o, NY),
            )
        )
    x_rows[x] = z_rows[:, :, :half]
    y_rows[y] = z_rows[:, :, half:]

    def ring_gather(axis, me, size, chunks, buf, sems, recvs):
        steps = size // 2

        def part(block, c, hop, way):
            ref = buf.at[block * chunks + c]
            if hop == steps:
                ref = ref.at[:, :quarter] if way == 0 else ref.at[:, quarter:]
            return ref

        def send(hop, way, c):
            sign = 1 - 2 * way
            ref = part(turn(me, -sign * (hop - 1), size), c, hop, way)
            at = ((hop - 1) * 2 + way) * chunks + c
            go(remote(ref, ref, sems.at[at], recvs.at[at], **{axis: turn(me, sign, size)}))

        def wait(hop, way, c):
            sign = 1 - 2 * way
            ref = part(turn(me, -sign * hop, size), c, hop, way)
            at = ((hop - 1) * 2 + way) * chunks + c
            remote(ref, ref, sems.at[at], recvs.at[at], **{axis: turn(me, sign, size)}).wait_recv()

        return send, wait

    def each(count):
        return [(c, way) for c in range(count) for way in range(2)]

    y_send, y_wait = ring_gather("y", y, NY, YC, ring_y, gry_send, gry_recv)
    x_send, x_wait = ring_gather("x", x, NX, XC, ring_x, grx_send, grx_recv)

    for o in range(1, NX):
        landed = x_rows.at[turn(x, -o, NX)]
        remote(landed, landed, gx_send.at[o - 1], gx_recv.at[o - 1], x=turn(x, o, NX)).wait_recv()
    for i in range(NX):
        for j in range(NZ):
            rows_f32[pl.ds((i * NZ + j) * 2, 2), :] = x_rows[i, j].astype(f32)
    for c in range(YC):
        ring_y[y * YC + c] = rows_f32[pl.ds(c * YR, YR), :].astype(bf16)
    for c, way in each(YC):
        y_send(1, way, c)

    for o in range(1, NY):
        landed = y_rows.at[turn(y, -o, NY)]
        remote(landed, landed, gy_send.at[o - 1], gy_recv.at[o - 1], y=turn(y, o, NY)).wait_recv()
    for i in range(NY):
        for j in range(NZ):
            rows_f32[pl.ds((i * NZ + j) * 2, 2), :] = y_rows[i, j].astype(f32)
    for c in range(XC):
        ring_x[x * XC + c] = rows_f32[pl.ds(c * XR, XR), :].astype(bf16)
    for c, way in each(XC):
        x_send(1, way, c)

    for c, way in each(YC):
        y_wait(1, way, c)
        y_send(2, way, c)
    for c, way in each(YC):
        y_wait(2, way, c)
        y_send(3, way, c)
        x_wait(1, way, c)
        x_send(2, way, c)
    for c, way in each(YC):
        y_wait(3, way, c)
        y_send(4, way, c)
    for c, way in each(XC):
        x_wait(2, way, c)
    for c, way in each(YC):
        y_wait(4, way, c)

    for copy in weights:
        copy.wait()
    rows_all = NX * NY * NZ * 2
    dims = (((1,), (1,)), ((), ()))

    def rows_of(ref):
        return ref[...].astype(f32).reshape(rows_all, half).astype(bf16)

    right = rows_of(ring_x)
    gate_r = lax.dot_general(right, w_gate[:, half:], dims, preferred_element_type=f32)
    up_r = lax.dot_general(right, w_up[:, half:], dims, preferred_element_type=f32)
    turned = perm[...].astype(f32)
    gate_r = jnp.dot(turned, gate_r, preferred_element_type=f32, precision=lax.Precision.HIGHEST)
    up_r = jnp.dot(turned, up_r, preferred_element_type=f32, precision=lax.Precision.HIGHEST)
    left = rows_of(ring_y)
    gate_act = gate_r + lax.dot_general(left, w_gate[:, :half], dims, preferred_element_type=f32)
    up_act = up_r + lax.dot_general(left, w_up[:, :half], dims, preferred_element_type=f32)
    hidden = (gate_act / (1.0 + jnp.exp(-gate_act)) * up_act).astype(bf16)
    hidden_t = jnp.dot(perm_t[...], hidden, preferred_element_type=f32).astype(bf16)

    def ring_sum(axis, me, size, chunks, parts, buf, landed, sems, recvs):
        steps = size // 2

        def cut(ref, hop, way):
            if hop == 1:
                ref = ref.at[:, :quarter] if way == 0 else ref.at[:, quarter:]
            return ref

        def copy(hop, way, c):
            sign = 1 - 2 * way
            at = ((hop - 1) * 2 + way) * chunks + c
            dest = turn(me, sign * (steps + 1 - hop), size)
            return remote(
                cut(buf.at[dest * chunks + c], hop, way),
                cut(landed.at[at], hop, way),
                sems.at[at],
                recvs.at[at],
                **{axis: turn(me, sign, size)},
            )

        def first(c):
            at = turn(me, steps, size) * chunks + c
            buf[at] = parts[at].astype(bf16)
            for way in range(2):
                go(copy(1, way, c))

        def add(hop, way, c):
            copy(hop, way, c).wait_recv()
            sign = 1 - 2 * way
            at = turn(me, sign * (steps - hop), size) * chunks + c
            got = landed.at[((hop - 1) * 2 + way) * chunks + c]
            if hop == 1:
                mine, other = (slice(0, quarter), slice(quarter, half))[:: 1 - 2 * way]
                buf[at, :, mine] = (parts[at, :, mine] + got[:, mine].astype(f32)).astype(bf16)
                buf[at, :, other] = parts[at, :, other].astype(bf16)
            else:
                buf[at] = (parts[at] + got[...].astype(f32)).astype(bf16)
            go(copy(hop + 1, way, c))

        def last(c):
            total = parts[me * chunks + c]
            for way in range(2):
                copy(steps, way, c).wait_recv()
                total = total + landed[((steps - 1) * 2 + way) * chunks + c].astype(f32)
            return total

        return first, add, last

    y_first, y_add, y_last = ring_sum(
        "y", y, NY, YC, part_y, send_y, recv_y, sry_send, sry_recv
    )
    x_first, x_add, x_last = ring_sum(
        "x", x, NX, XC, part_x, send_x, recv_x, srx_send, srx_recv
    )

    part_y[...] = jnp.dot(hidden, w_down[:, :half], preferred_element_type=f32).reshape(part_y.shape)
    for c in range(YC):
        y_first(c)
    part_x[...] = jnp.dot(hidden_t, w_down[:, half:], preferred_element_type=f32).reshape(part_x.shape)
    for c in range(XC):
        x_first(c)
    for c, way in each(YC):
        y_add(1, way, c)
    for c, way in each(YC):
        y_add(2, way, c)
        x_add(1, way, c)
    for c, way in each(YC):
        y_add(3, way, c)

    for c in range(XC):
        flat_f32[pl.ds(c * XR, XR), :] = x_last(c)
    for i in range(NY):
        for j in range(NZ):
            rows = flat_f32[pl.ds((i * NZ + j) * 2, 2), :]
            mid_y_f32[i, j] = rows
            mid_y[i, j] = rows.astype(bf16)
    for o in range(1, NY):
        go(
            remote(
                mid_y.at[turn(y, o, NY)],
                mid_y_recv.at[o - 1],
                sy_send.at[o - 1],
                sy_recv.at[o - 1],
                y=turn(y, o, NY),
            )
        )
    for c in range(YC):
        flat_f32[pl.ds(c * YR, YR), :] = y_last(c)
    for i in range(NX):
        for j in range(NZ):
            rows = flat_f32[pl.ds((i * NZ + j) * 2, 2), :]
            mid_x_f32[i, j] = rows
            mid_x[i, j] = rows.astype(bf16)
    for o in range(1, NX):
        go(
            remote(
                mid_x.at[turn(x, o, NX)],
                mid_x_recv.at[o - 1],
                sx_send.at[o - 1],
                sx_recv.at[o - 1],
                x=turn(x, o, NX),
            )
        )

    total = mid_y_f32[y]
    for o in range(1, NY):
        landed = mid_y_recv.at[o - 1]
        remote(landed, landed, sy_send.at[o - 1], sy_recv.at[o - 1], y=turn(y, o, NY)).wait_recv()
        total = total + landed[...].astype(f32)
    mid_z_f32[:, :, half:] = total
    mid_z[:, :, half:] = total.astype(bf16)
    total = mid_x_f32[x]
    for o in range(1, NX):
        landed = mid_x_recv.at[o - 1]
        remote(landed, landed, sx_send.at[o - 1], sx_recv.at[o - 1], x=turn(x, o, NX)).wait_recv()
        total = total + landed[...].astype(f32)
    mid_z_f32[:, :, :half] = total
    mid_z[:, :, :half] = total.astype(bf16)
    for o in range(1, NZ):
        go(
            remote(
                mid_z.at[turn(z, o, NZ)],
                mid_z_recv.at[o - 1],
                sz_send.at[o - 1],
                sz_recv.at[o - 1],
                z=turn(z, o, NZ),
            )
        )
    total = mid_z_f32[z]
    for o in range(1, NZ):
        landed = mid_z_recv.at[o - 1]
        remote(landed, landed, sz_send.at[o - 1], sz_recv.at[o - 1], z=turn(z, o, NZ)).wait_recv()
        total = total + landed[...].astype(f32)
    out[0] = total

    for copy in sent:
        copy.wait_send()


def swap_matrix():
    k = np.arange(NY * NX * NZ * 2)
    per = NZ * 2
    i, j, q = k // (per * NX), k // per % NX, k % per
    table = np.zeros((k.size, k.size), np.float32)
    table[k, (j * NY + i) * per + q] = 1
    return table


def experts(picked, w_gate, w_up, w_down):
    width = picked.shape[-1]
    half = width // 2
    bf16, f32 = jnp.bfloat16, jnp.float32
    rows = NX * NY * NZ * 2
    table = swap_matrix()
    dma = pltpu.SemaphoreType.DMA
    vmem = pltpu.VMEM
    ring = lambda n, c: n // 2 * 2 * c
    weight = vmem(w_gate.shape[1:], bf16)
    scratch = [
        weight,
        weight,
        weight,
        vmem((NZ, 2, width), bf16),
        vmem((NX, NZ, 2, half), bf16),
        vmem((NY, NZ, 2, half), bf16),
        vmem((NY * NZ * 2, half), f32),
        vmem((NY * YC, YR, half), bf16),
        vmem((NX * XC, XR, half), bf16),
        vmem((NY * YC, YR, half), f32),
        vmem((NX * XC, XR, half), f32),
        vmem((NY * YC, YR, half), bf16),
        vmem((NX * XC, XR, half), bf16),
        vmem((ring(NY, YC), YR, half), bf16),
        vmem((ring(NX, XC), XR, half), bf16),
        vmem((NY * NZ * 2, half), f32),
        vmem((NX, NZ, 2, half), f32),
        vmem((NX, NZ, 2, half), bf16),
        vmem((NX - 1, NZ, 2, half), bf16),
        vmem((NY, NZ, 2, half), f32),
        vmem((NY, NZ, 2, half), bf16),
        vmem((NY - 1, NZ, 2, half), bf16),
        vmem((NZ, 2, width), f32),
        vmem((NZ, 2, width), bf16),
        vmem((NZ - 1, 2, width), bf16),
        dma((3,)),
    ]
    for count in (NZ - 1, NX - 1, NY - 1, ring(NY, YC), ring(NX, XC), ring(NY, YC), ring(NX, XC), NX - 1, NY - 1, NZ - 1):
        scratch += [dma((count,)), dma((count,))]
    in_vmem = pl.BlockSpec(memory_space=pltpu.VMEM)
    in_hbm = pl.BlockSpec(memory_space=pl.ANY)
    return pl.pallas_call(
        experts_kernel,
        out_shape=jax.ShapeDtypeStruct((1, 2, width), f32),
        in_specs=[in_vmem, in_hbm, in_hbm, in_hbm, in_vmem, in_vmem],
        out_specs=in_vmem,
        scratch_shapes=scratch,
        compiler_params=pltpu.CompilerParams(
            collective_id=0, has_side_effects=True, vmem_limit_bytes=56 * 1024 * 1024
        ),
        name="experts",
    )(
        picked,
        w_gate,
        w_up,
        w_down,
        jnp.asarray(table, bf16),
        jnp.asarray(table.T, bf16),
    )


def sent_to_all(array, axis):
    copies = jnp.broadcast_to(array, (lax.axis_size(axis), *array.shape))
    return lax.all_to_all(copies, axis, split_axis=0, concat_axis=0, tiled=True)


def collect(array, axis):
    blocks = sent_to_all(array, axis)
    return blocks.reshape(-1, *array.shape[1:])


def on_device(tokens, select, gates, gate_proj, up_proj, down_proj):
    groups = lax.axis_size("grp")
    tok_dev, width = tokens.shape
    slots = select.shape[1]
    first = (lax.axis_index(BLK) * groups + lax.axis_index("grp")) * tok_dev
    local_ids = collect(select, "grp").reshape(-1) - first
    owned = (local_ids[:, None] == jnp.arange(tok_dev, dtype=jnp.int32)[None, :]).astype(
        jnp.bfloat16
    )
    candidates = jnp.dot(owned, tokens, preferred_element_type=jnp.float32)
    arrived = lax.all_to_all(
        candidates.astype(jnp.bfloat16), "grp", split_axis=0, concat_axis=0, tiled=True
    )
    picked = jnp.sum(arrived.reshape(groups, slots, width).astype(jnp.float32), axis=0).astype(
        jnp.bfloat16
    )
    summed = experts(picked[None], gate_proj, up_proj, down_proj)[0]
    expert_out = summed.astype(jnp.bfloat16)
    weighted = (gates[0][:, None] * expert_out.astype(jnp.float32)).astype(jnp.bfloat16)
    mixed = jnp.dot(owned.T, collect(weighted, "grp"), preferred_element_type=jnp.float32)
    return mixed.astype(jnp.bfloat16)


def solution(mesh):
    finer = Mesh(mesh.devices.reshape(NY, NZ, NX, mesh.shape["grp"]), BLK_GRP)
    in_specs = (
        P(BLK_GRP, None),
        P("grp", BLK),
        P("grp", BLK),
        P("grp", BLK, None),
        P("grp", BLK, None),
        P("grp", BLK, None),
    )
    return jax.shard_map(
        on_device, mesh=finer, in_specs=in_specs, out_specs=P(BLK_GRP, None), check_vma=False
    )
```

time: 747 us -> 119 us (0.16)
  waiting for transfers between devices: 494 us -> 9.34 us
  blocking collectives: 199 us -> 35.9 us
  Pallas kernels: 0 us -> 50.6 us
  between operations: 13.5 us -> 0.05 us
  local copies, waits for them, and re-layouts: 13.9 us -> 1.67 us
    reduce_scatter x1 -> x0, waiting for transfers between devices: 447 us -> none  [sum_in_tiles(): lax.psum_scatter(padded.reshape(-1, 128), axis, scatter_dimension=0, tile...]
    all_to_all x1, blocking collectives: 154 us -> 22.5 us  [sent_to_all(): return lax.all_to_all(copies, axis, split_axis=0, concat_axis=0, tiled=True)]
    pallas_call x0 -> x1, Pallas kernels: none -> 50.6 us  [experts(): pl.pallas_call(experts_kernel, out_shape=jax.ShapeDtypeStruct((1, 2, widt...]
    all_gather x1 -> x0, waiting for transfers between devices: 38 us -> none  [all_blocks(): blocks = lax.all_gather(blocks, axes[k])]
    all_gather x2 -> x0, blocking collectives: 31.1 us -> none  [all_blocks(): blocks = lax.all_gather(blocks, axes[k])]
  transfers between devices with their start and end apart: 3 -> 1, of which waited for: 3 -> 1; matrix products, arithmetic and copies ran while one was open for 0% -> 0% of each run, Pallas kernels for 0% -> 0%
where the time goes in v1:
time: 119 us; the launch traced here: 117 us
  Pallas kernels  50.6 us (43%)
  blocking collectives  35.9 us (30%)
  starting transfers between devices  16 us (13%)
  waiting for transfers between devices  9.34 us (8%)
  matrix products  1.81 us (2%)
  local copies, waits for them, and re-layouts  1.67 us (1%)
  other arithmetic  1.58 us (1%)
    pallas_call x1, Pallas kernels, experts(): pl.pallas_call(experts_kernel, out_shape=jax.ShapeDtypeStruct((1, 2, widt...  50.6 us
    all_to_all x1, blocking collectives, sent_to_all(): return lax.all_to_all(copies, axis, split_axis=0, concat_axis=0, tiled=True)  22.5 us
    all_to_all x1, starting transfers between devices, sent_to_all(): return lax.all_to_all(copies, axis, split_axis=0, concat_axis=0, tiled=True)  16 us
    all_to_all x1, blocking collectives, on_device(): lax.all_to_all(candidates.astype(jnp.bfloat16), 'grp', split_axis=0, conc...  13.5 us
    all_to_all x1, waiting for transfers between devices, sent_to_all(): return lax.all_to_all(copies, axis, split_axis=0, concat_axis=0, tiled=True)  9.34 us
  transfers between devices with their start and end apart: 1, of which 1 were waited for; matrix products, arithmetic and copies ran while one was open for 0% of the time, Pallas kernels for 0%

profile of v1, /device:TPU:1, one launch (start us, length us, event | category | flops | bytes accessed | tf_op | source)
XLA Modules:
  0.0 117.0 jit_solution(18282011122073704355)
XLA Ops:
  0.0 0.0 copy-start
  0.0 1.3 %broadcast_in_dim.11 = s32[8,1,2]{2,1,0:T(1,128)} broadcast(s32[2]{0:T(128)} %bitcast.10), dimensions={2} | broadcast | bytes 72 | tf_op jit(solution)/shard_map/broadcast_in_dim | solution.py:446
  1.3 16.0 %all-to-all-start = ((s32[8,1,2]{2,1,0:T(1,128)}), s32[8,1,2]{2,1,0:T(1,128)S(1)}, u32[]{:S(2)}, u32[]{:S(2)}) async-start(s32[8,1,2]{2,1,0:T(1,128)} %broadcast_in_dim.11), calls=%async_computation | async-start | bytes 8192 | tf_op jit(solution)/shard_map/all_to_all | solution.py:447
  17.3 9.3 %all-to-all-done = s32[8,1,2]{2,1,0:T(1,128)S(1)} async-done(((s32[8,1,2]{2,1,0:T(1,128)}), s32[8,1,2]{2,1,0:T(1,128)S(1)}, u32[]{:S(2)}, u32[]{:S(2)}) %all-to-all-start) | async-done | bytes 96 | tf_op jit(solution)/shard_map/all_to_all | solution.py:447
  26.7 0.1 sub.15
  26.8 0.0 copy-done
  26.8 0.3 convolution_convert_fusion.1
  27.1 0.1 all_to_all.13
  27.2 13.5 %all_to_all.19 = bf16[8,2,4096]{2,1,0:T(2,128)(2,1)S(1)} all-to-all(bf16[8,2,4096]{2,1,0:T(2,128)(2,1)S(1)} %all_to_all.13), channel_id=1, replica_groups=mesh['y'=8,'z'=3,'x'=4,'grp'=8] {'grp'}, dimensions={0} | all-to-all | bytes 262144 | tf_op jit(solution)/shard_map/all_to_all | solution.py:465
  40.7 0.7 reduce_sum.12
  41.4 0.0 copy-start.1
  41.4 50.6 %experts.1 = f32[1,2,4096]{2,1,0:T(2,128)} custom-call(bf16[1,2,4096]{2,1,0:T(2,128)(2,1)} %bitcast.8, bf16[1,112,4096]{2,1,0:T(8,128)(2,1)} %w_gate_hbm.1, bf16[1,112,4096]{2,1,0:T(8,128)(2,1)} %w_up_hbm.1, bf16[1,112,4096]{2,1,0:T(8,128)(2,1)} %w_down_hbm.1, bf16[192,192]{1,0:T(8,128)(2,1)} %constant.30.clone.perm, bf16[192,192]{1,0:T(8,128)(2,1)} %constant.31.clone.perm_t), custom_call_target="tpu_custom_call" | custom-call | tf_op jit(solution)/shard_map/experts/pallas_call | solution.py:425
  92.0 0.0 copy-done.1
  92.0 0.8 fusion
  92.8 0.1 broadcast_in_dim.13
  92.9 22.5 %all_to_all.20 = bf16[8,2,4096]{2,1,0:T(2,128)(2,1)S(1)} all-to-all(bf16[8,2,4096]{2,1,0:T(2,128)(2,1)S(1)} %broadcast_in_dim.13), channel_id=1, replica_groups=mesh['y'=8,'z'=3,'x'=4,'grp'=8] {'grp'}, dimensions={0} | all-to-all | bytes 262144 | tf_op jit(solution)/shard_map/all_to_all | solution.py:447
  115.4 0.1 reshape.19
  115.4 1.5 %convolution_convert_fusion = bf16[128,4096]{1,0:T(8,128)(2,1)} fusion(bf16[16,4096]{1,0:T(8,128)(2,1)S(1)} %reshape.19, s32[16]{0:T(128)S(1)} %sub.15), kind=kOutput, calls=%fused_computation | convolution fusion | flops 17303552 | bytes 1179712 | tf_op jit(solution)/shard_map/dot_general | solution.py:474
  (1 shorter events, 0.0 us)
Async XLA Ops:
  0.0 26.8 %copy-start = (bf16[128,4096]{1,0:T(8,128)(2,1)S(1)}, bf16[128,4096]{1,0:T(8,128)(2,1)}, u32[]{:S(2)}) copy-start(bf16[128,4096]{1,0:T(8,128)(2,1)} %param.8) | copy-start | bytes 3145732
  1.3 25.3 %all-to-all-start = ((s32[8,1,2]{2,1,0:T(1,128)}), s32[8,1,2]{2,1,0:T(1,128)S(1)}, u32[]{:S(2)}, u32[]{:S(2)}) async-start(s32[8,1,2]{2,1,0:T(1,128)} %broadcast_in_dim.11), calls=%async_computation | async-start | bytes 8192 | tf_op jit(solution)/shard_map/all_to_all | solution.py:447
  41.4 50.6 %copy-start.1 = (f32[1,2]{1,0:T(1,128)S(1)}, f32[1,2]{1,0:T(1,128)}, u32[]{:S(2)}) copy-start(f32[1,2]{1,0:T(1,128)} %param.10) | copy-start | bytes 28

commit v2 on v0

v2 whole, which is shorter than its diff:
```python
import jax
import jax.numpy as jnp
import numpy as np
from jax import lax
from jax.experimental import pallas as pl
from jax.experimental.pallas import tpu as pltpu
from jax.sharding import Mesh
from jax.sharding import PartitionSpec as P

BLK = ("y", "z", "x")
BLK_GRP = ("y", "z", "x", "grp")
NY, NZ, NX = 8, 3, 4
NH, NC = 4, 2
NG = NH * NC
YC, XC = 3, 3
YR, XR = NX * NZ * 2 // YC, NY * NZ * 2 // XC
ROWS = NX * NY * NZ * 2
FAR_FIRST = [(h, c) for h in (2, 1, 3, 0) for c in range(NC) if h or c]
LEFT, RIGHT = 0, 1


def remote(src, dst, send_sem, recv_sem, **where):
    return pltpu.make_async_remote_copy(
        src_ref=src,
        dst_ref=dst,
        send_sem=send_sem,
        recv_sem=recv_sem,
        device_id=where,
        device_id_type=pl.DeviceIdType.MESH,
    )


def turn(index, by, size):
    return lax.rem(index + by + size, size)


def each(count):
    return [(c, way) for c in range(count) for way in range(2)]


def ring_gather(go, axis, me, size, chunks, buf, sems, recvs):
    steps = size // 2
    middle = buf.shape[-1] // 2

    def copy(block, hop, way, c):
        ref = buf.at[block * chunks + c]
        if hop == steps:
            ref = ref.at[:, :middle] if way == 0 else ref.at[:, middle:]
        at = ((hop - 1) * 2 + way) * chunks + c
        return remote(ref, ref, sems.at[at], recvs.at[at], **{axis: turn(me, 1 - 2 * way, size)})

    def send(hop, way, c):
        go(copy(turn(me, (2 * way - 1) * (hop - 1), size), hop, way, c))

    def wait(hop, way, c):
        copy(turn(me, (2 * way - 1) * hop, size), hop, way, c).wait_recv()

    return send, wait


def ring_sum(go, axis, me, size, chunks, parts, buf, landed, sems, recvs):
    steps = size // 2
    half = buf.shape[-1]
    middle = half // 2
    f32, bf16 = jnp.float32, jnp.bfloat16

    def cut(ref, hop, way):
        if hop == 1:
            ref = ref.at[:, :middle] if way == 0 else ref.at[:, middle:]
        return ref

    def copy(hop, way, c):
        sign = 1 - 2 * way
        at = ((hop - 1) * 2 + way) * chunks + c
        dest = turn(me, sign * (steps + 1 - hop), size)
        return remote(
            cut(buf.at[dest * chunks + c], hop, way),
            cut(landed.at[at], hop, way),
            sems.at[at],
            recvs.at[at],
            **{axis: turn(me, sign, size)},
        )

    def first(c):
        at = turn(me, steps, size) * chunks + c
        buf[at] = parts[at].astype(bf16)
        for way in range(2):
            go(copy(1, way, c))

    def add(hop, way, c):
        copy(hop, way, c).wait_recv()
        at = turn(me, (1 - 2 * way) * (steps - hop), size) * chunks + c
        got = landed.at[((hop - 1) * 2 + way) * chunks + c]
        if hop == 1:
            mine, other = (slice(0, middle), slice(middle, half))[:: 1 - 2 * way]
            buf[at, :, mine] = (parts[at, :, mine] + got[:, mine].astype(f32)).astype(bf16)
            buf[at, :, other] = parts[at, :, other].astype(bf16)
        else:
            buf[at] = (parts[at] + got[...].astype(f32)).astype(bf16)
        go(copy(hop + 1, way, c))

    def last(c):
        total = parts[me * chunks + c]
        for way in range(2):
            copy(steps, way, c).wait_recv()
            total = total + landed[((steps - 1) * 2 + way) * chunks + c].astype(f32)
        return total

    return first, add, last


def layer_kernel(
    ids,
    gates,
    perm,
    perm_t,
    tokens_hbm,
    gate_hbm,
    up_hbm,
    down_hbm,
    rows_out,
    owned_out,
    tokens,
    w_in,
    w_out,
    all_ids,
    owned,
    cand_f32,
    cand,
    arrived,
    z_rows,
    x_rows,
    y_rows,
    flat_f32,
    ring_y,
    ring_x,
    part_y,
    part_x,
    sum_y,
    sum_x,
    got_y,
    got_x,
    mid_x_f32,
    mid_x,
    mid_x_got,
    mid_y_f32,
    mid_y,
    mid_y_got,
    mid_z,
    mid_z_got,
    weighted,
    gathered,
    w_sem,
    *sems,
):
    y, z, x = lax.axis_index("y"), lax.axis_index("z"), lax.axis_index("x")
    g = lax.axis_index("grp")
    chip, core = g // NC, lax.rem(g, NC)
    tok_dev, width = tokens.shape
    half = width // 2
    hid = gate_hbm.shape[1]
    pad = w_out.shape[0]
    cols = (slice(0, half), slice(half, width))
    f32, bf16 = jnp.float32, jnp.bfloat16
    (
        (id_send, id_recv),
        (row_send, row_recv),
        (gz_send, gz_recv),
        (gx_send, gx_recv),
        (gy_send, gy_recv),
        ring_gy,
        ring_gx,
        ring_sy,
        ring_sx,
        (sx_send, sx_recv),
        (sy_send, sy_recv),
        (sz_send, sz_recv),
        (out_send, out_recv),
    ) = zip(sems[::2], sems[1::2])
    sent = []

    def go(copy):
        copy.start()
        sent.append(copy)

    def peer(h, c, sign=1):
        return turn(chip, sign * h, NH) * NC + turn(core, sign * c, NC)

    loads = [
        pltpu.make_async_copy(tokens_hbm, tokens, w_sem.at[0]),
        pltpu.make_async_copy(gate_hbm.at[0], w_in.at[pl.ds(0, hid)], w_sem.at[1]),
        pltpu.make_async_copy(up_hbm.at[0], w_in.at[pl.ds(pad, hid)], w_sem.at[2]),
        pltpu.make_async_copy(down_hbm.at[0], w_out.at[pl.ds(0, hid)], w_sem.at[3]),
    ]
    for copy in loads:
        copy.start()

    barrier = pltpu.get_barrier_semaphore()
    for h, c in FAR_FIRST:
        pl.semaphore_signal(barrier, device_id={"grp": peer(h, c)})
    for o in range(1, NY):
        pl.semaphore_signal(barrier, device_id={"y": turn(y, o, NY)})
    for o in range(1, NX):
        pl.semaphore_signal(barrier, device_id={"x": turn(x, o, NX)})
    for o in range(1, NZ):
        pl.semaphore_signal(barrier, device_id={"z": turn(z, o, NZ)})
    pl.semaphore_wait(barrier, NG + NZ + NX + NY - 4)

    for h, c in FAR_FIRST:
        at = h * NC + c
        go(remote(ids, all_ids.at[g], id_send.at[at], id_recv.at[at], grp=peer(h, c)))
    all_ids[g] = ids[...]
    for at in (hid, pad + hid):
        w_in[pl.ds(at, pad - hid), :] = jnp.zeros((pad - hid, width), bf16)
    w_out[pl.ds(hid, pad - hid), :] = jnp.zeros((pad - hid, width), bf16)
    loads[0].wait()
    for h, c in FAR_FIRST[::-1]:
        at, landed = h * NC + c, all_ids.at[peer(h, c, -1)]
        remote(landed, landed, id_send.at[at], id_recv.at[at], grp=peer(h, c)).wait_recv()

    block = (y * NZ + z) * NX + x
    lane = lax.broadcasted_iota(jnp.int32, (2, tok_dev), 1) + (block * NG + g) * tok_dev
    for e in range(NG):
        owned[pl.ds(e * 2, 2), :] = (all_ids[e] == lane).astype(f32)
    chosen = owned[...].astype(bf16)
    for k in (RIGHT, LEFT):
        cand_f32[...] = jnp.dot(chosen, tokens[:, cols[k]], preferred_element_type=f32)
        for e in range(NG):
            cand[k, e] = cand_f32[pl.ds(e * 2, 2), :].astype(bf16)
        for h, c in FAR_FIRST:
            at, to = h * NC + c, peer(h, c)
            go(
                remote(
                    cand.at[k, to],
                    arrived.at[k, at],
                    row_send.at[k * NG + at],
                    row_recv.at[k * NG + at],
                    grp=to,
                )
            )

    def spread(k, o):
        src = z_rows.at[k, turn(z, -o, NZ)]
        axis, me, size, buf, send, recv = (
            ("x", x, NX, x_rows, gx_send, gx_recv),
            ("y", y, NY, y_rows, gy_send, gy_recv),
        )[k]
        for d in range(1, size):
            at = o * (size - 1) + d - 1
            dst = buf.at[me, turn(z, -o, NZ)]
            go(remote(src, dst, send.at[at], recv.at[at], **{axis: turn(me, d, size)}))
        buf[me, turn(z, -o, NZ)] = src[...]

    def spread_wait(k):
        axis, me, size, buf, send, recv = (
            ("x", x, NX, x_rows, gx_send, gx_recv),
            ("y", y, NY, y_rows, gy_send, gy_recv),
        )[k]
        for o in range(NZ):
            for d in range(1, size):
                at = o * (size - 1) + d - 1
                landed = buf.at[turn(me, -d, size), turn(z, -o, NZ)]
                remote(
                    landed, landed, send.at[at], recv.at[at], **{axis: turn(me, d, size)}
                ).wait_recv()

    for k in (RIGHT, LEFT):
        total = cand[k, g].astype(f32)
        for h, c in FAR_FIRST[::-1]:
            at = h * NC + c
            landed = arrived.at[k, at]
            remote(
                landed, landed, row_send.at[k * NG + at], row_recv.at[k * NG + at], grp=peer(h, c)
            ).wait_recv()
            total = total + landed[...].astype(f32)
        z_rows[k, z] = total.astype(bf16)
        for o in range(1, NZ):
            at = k * (NZ - 1) + o - 1
            ref = z_rows.at[k, z]
            go(remote(ref, ref, gz_send.at[at], gz_recv.at[at], z=turn(z, o, NZ)))
        spread(k, 0)
    for k in (RIGHT, LEFT):
        for o in range(1, NZ):
            at = k * (NZ - 1) + o - 1
            landed = z_rows.at[k, turn(z, -o, NZ)]
            remote(landed, landed, gz_send.at[at], gz_recv.at[at], z=turn(z, o, NZ)).wait_recv()
            spread(k, o)

    y_send, y_wait = ring_gather(go, "y", y, NY, YC, ring_y, *ring_gy)
    x_send, x_wait = ring_gather(go, "x", x, NX, XC, ring_x, *ring_gx)

    spread_wait(LEFT)
    for i in range(NX):
        for j in range(NZ):
            flat_f32[pl.ds((i * NZ + j) * 2, 2), :] = x_rows[i, j].astype(f32)
    for c in range(YC):
        ring_y[y * YC + c] = flat_f32[pl.ds(c * YR, YR), :].astype(bf16)
    for c, way in each(YC):
        y_send(1, way, c)
    spread_wait(RIGHT)
    for i in range(NY):
        for j in range(NZ):
            flat_f32[pl.ds((i * NZ + j) * 2, 2), :] = y_rows[i, j].astype(f32)
    for c in range(XC):
        ring_x[x * XC + c] = flat_f32[pl.ds(c * XR, XR), :].astype(bf16)
    for c, way in each(XC):
        x_send(1, way, c)
    for c, way in each(YC):
        y_wait(1, way, c)
        y_send(2, way, c)
    for c, way in each(YC):
        y_wait(2, way, c)
        y_send(3, way, c)
        x_wait(1, way, c)
        x_send(2, way, c)
    for c, way in each(YC):
        y_wait(3, way, c)
        y_send(4, way, c)
    for copy in loads[1:]:
        copy.wait()
    for c, way in each(XC):
        x_wait(2, way, c)

    def from_ring(ref, k):
        rows = ref[...].astype(f32).reshape(ROWS, half).astype(bf16)
        return lax.dot_general(
            rows, w_in[:, cols[k]], (((1,), (1,)), ((), ())), preferred_element_type=f32
        )

    act = from_ring(ring_x, RIGHT)
    high = act.astype(bf16)
    rest = act - high.astype(f32)
    middle = rest.astype(bf16)
    low = (rest - middle.astype(f32)).astype(bf16)
    act = sum(jnp.dot(perm[...], term, preferred_element_type=f32) for term in (low, middle, high))
    for c, way in each(YC):
        y_wait(4, way, c)
    act = act + from_ring(ring_y, LEFT)
    gate_act, up_act = act[:, :pad], act[:, pad:]
    hidden = (gate_act / (1.0 + jnp.exp(-gate_act)) * up_act).astype(bf16)

    y_first, y_add, y_last = ring_sum(go, "y", y, NY, YC, part_y, sum_y, got_y, *ring_sy)
    x_first, x_add, x_last = ring_sum(go, "x", x, NX, XC, part_x, sum_x, got_x, *ring_sx)

    part_y[...] = jnp.dot(hidden, w_out[:, :half], preferred_element_type=f32).reshape(part_y.shape)
    for c in range(YC):
        y_first(c)
    hidden_t = jnp.dot(perm_t[...], hidden, preferred_element_type=f32).astype(bf16)
    part_x[...] = jnp.dot(hidden_t, w_out[:, half:], preferred_element_type=f32).reshape(part_x.shape)
    for c in range(XC):
        x_first(c)
    for c, way in each(YC):
        y_add(1, way, c)
    for c, way in each(YC):
        y_add(2, way, c)
        x_add(1, way, c)
    for c, way in each(YC):
        y_add(3, way, c)

    mids = (
        ("x", x, NX, mid_x_f32, mid_x, mid_x_got, sx_send, sx_recv),
        ("y", y, NY, mid_y_f32, mid_y, mid_y_got, sy_send, sy_recv),
    )

    def back(k, last, chunks, height):
        axis, me, size, wide, buf, got, send, recv = mids[k]
        for c in range(chunks):
            flat_f32[pl.ds(c * height, height), :] = last(c)
        for i in range(size):
            for j in range(NZ):
                rows = flat_f32[pl.ds((i * NZ + j) * 2, 2), :]
                wide[i, j] = rows
                buf[i, j] = rows.astype(bf16)
        for o in (1, 2, 0):
            for d in range(1, size):
                at = o * (size - 1) + d - 1
                src = buf.at[turn(me, d, size), turn(z, o, NZ)]
                go(remote(src, got.at[at], send.at[at], recv.at[at], **{axis: turn(me, d, size)}))

    def back_sum(k, o):
        axis, me, size, wide, buf, got, send, recv = mids[k]
        total = wide[me, turn(z, o, NZ)]
        for d in range(1, size):
            at = o * (size - 1) + d - 1
            landed = got.at[at]
            remote(
                landed, landed, send.at[at], recv.at[at], **{axis: turn(me, d, size)}
            ).wait_recv()
            total = total + landed[...].astype(f32)
        return total

    back(RIGHT, x_last, XC, XR)
    back(LEFT, y_last, YC, YR)
    for k in (LEFT, RIGHT):
        for o in range(1, NZ):
            at = k * (NZ - 1) + o - 1
            mid_z[at] = back_sum(k, o).astype(bf16)
            go(
                remote(
                    mid_z.at[at], mid_z_got.at[at], sz_send.at[at], sz_recv.at[at], z=turn(z, o, NZ)
                )
            )
    for k in (LEFT, RIGHT):
        total = back_sum(k, 0)
        for o in range(1, NZ):
            at = k * (NZ - 1) + o - 1
            landed = mid_z_got.at[at]
            remote(landed, landed, sz_send.at[at], sz_recv.at[at], z=turn(z, o, NZ)).wait_recv()
            total = total + landed[...].astype(f32)
        weighted[k] = (gates[:, :1] * total.astype(bf16).astype(f32)).astype(bf16)
        for h, c in FAR_FIRST:
            at = k * NG + h * NC + c
            go(
                remote(
                    weighted.at[k], gathered.at[k, g], out_send.at[at], out_recv.at[at], grp=peer(h, c)
                )
            )
        gathered[k, g] = weighted[k]

    owned_out[...] = chosen
    for k in (LEFT, RIGHT):
        for h, c in FAR_FIRST[::-1]:
            at = k * NG + h * NC + c
            landed = gathered.at[k, peer(h, c, -1)]
            remote(landed, landed, out_send.at[at], out_recv.at[at], grp=peer(h, c)).wait_recv()
        rows_out[:, :, cols[k]] = gathered[k]
    for copy in sent:
        copy.wait_send()


def swap_matrix():
    k = np.arange(ROWS)
    per = NZ * 2
    i, j, q = k // (per * NX), k // per % NX, k % per
    table = np.zeros((ROWS, ROWS), np.float32)
    table[k, (j * NY + i) * per + q] = 1
    return table


def on_device(tokens, select, gates, gate_proj, up_proj, down_proj):
    tok_dev, width = tokens.shape
    half = width // 2
    bf16, f32 = jnp.bfloat16, jnp.float32
    dma, vmem = pltpu.SemaphoreType.DMA, pltpu.VMEM
    hops_y, hops_x = NY * YC, NX * XC
    pad = -(-gate_proj.shape[1] // 128) * 128
    scratch = [
        vmem((tok_dev, width), bf16),
        vmem((2 * pad, width), bf16),
        vmem((pad, width), bf16),
        vmem((NG, 2, tok_dev), jnp.int32),
        vmem((NG * 2, tok_dev), f32),
        vmem((NG * 2, half), f32),
        vmem((2, NG, 2, half), bf16),
        vmem((2, NG, 2, half), bf16),
        vmem((2, NZ, 2, half), bf16),
        vmem((NX, NZ, 2, half), bf16),
        vmem((NY, NZ, 2, half), bf16),
        vmem((NY * NZ * 2, half), f32),
        vmem((NY * YC, YR, half), bf16),
        vmem((NX * XC, XR, half), bf16),
        vmem((NY * YC, YR, half), f32),
        vmem((NX * XC, XR, half), f32),
        vmem((NY * YC, YR, half), bf16),
        vmem((NX * XC, XR, half), bf16),
        vmem((hops_y, YR, half), bf16),
        vmem((hops_x, XR, half), bf16),
        vmem((NX, NZ, 2, half), f32),
        vmem((NX, NZ, 2, half), bf16),
        vmem((NZ * (NX - 1), 2, half), bf16),
        vmem((NY, NZ, 2, half), f32),
        vmem((NY, NZ, 2, half), bf16),
        vmem((NZ * (NY - 1), 2, half), bf16),
        vmem((2 * (NZ - 1), 2, half), bf16),
        vmem((2 * (NZ - 1), 2, half), bf16),
        vmem((2, 2, half), bf16),
        vmem((2, NG, 2, half), bf16),
        dma((4,)),
    ]
    for count in (
        NG,
        2 * NG,
        2 * (NZ - 1),
        NZ * (NX - 1),
        NZ * (NY - 1),
        hops_y,
        hops_x,
        hops_y,
        hops_x,
        NZ * (NX - 1),
        NZ * (NY - 1),
        2 * (NZ - 1),
        2 * NG,
    ):
        scratch += [dma((count,)), dma((count,))]
    in_vmem = pl.BlockSpec(memory_space=pltpu.VMEM)
    in_hbm = pl.BlockSpec(memory_space=pl.ANY)
    table = swap_matrix()
    rows, owned = pl.pallas_call(
        layer_kernel,
        out_shape=(
            jax.ShapeDtypeStruct((NG, 2, width), bf16),
            jax.ShapeDtypeStruct((NG * 2, tok_dev), bf16),
        ),
        in_specs=[in_vmem] * 4 + [in_hbm] * 4,
        out_specs=(in_vmem, in_vmem),
        scratch_shapes=scratch,
        compiler_params=pltpu.CompilerParams(
            collective_id=0, has_side_effects=True, vmem_limit_bytes=56 * 1024 * 1024
        ),
        name="layer",
    )(
        jnp.broadcast_to(select.reshape(2, 1), (2, tok_dev)),
        jnp.broadcast_to(gates.reshape(2, 1), (2, 128)),
        jnp.asarray(table, bf16),
        jnp.asarray(table.T, bf16),
        tokens,
        gate_proj,
        up_proj,
        down_proj,
    )
    mixed = jnp.dot(owned.T, rows.reshape(NG * 2, width), preferred_element_type=f32)
    return mixed.astype(bf16)


def solution(mesh):
    finer = Mesh(mesh.devices.reshape(NY, NZ, NX, NG), BLK_GRP)
    in_specs = (
        P(BLK_GRP, None),
        P("grp", BLK),
        P("grp", BLK),
        P("grp", BLK, None),
        P("grp", BLK, None),
        P("grp", BLK, None),
    )
    return jax.shard_map(
        on_device, mesh=finer, in_specs=in_specs, out_specs=P(BLK_GRP, None), check_vma=False
    )
```

time: 747 us -> 96.7 us (0.13)
  waiting for transfers between devices: 494 us -> 0 us
  blocking collectives: 199 us -> 0 us
  Pallas kernels: 0 us -> 90.8 us
  starting transfers between devices: 16 us -> 0 us
  between operations: 13.5 us -> 0.01 us
  local copies, waits for them, and re-layouts: 13.9 us -> 3.52 us
    reduce_scatter x1 -> x0, waiting for transfers between devices: 447 us -> none  [sum_in_tiles(): lax.psum_scatter(padded.reshape(-1, 128), axis, scatter_dimension=0, tile...]
    all_to_all x2 -> x0, blocking collectives: 168 us -> none  [the longest x1 154 us: sent_to_all(): return lax.all_to_all(copies, axis, split_axis=0, concat_axis=0, tiled=True)]
    pallas_call x0 -> x1, Pallas kernels: none -> 90.8 us  [on_device(): pl.pallas_call(layer_kernel, out_shape=(jax.ShapeDtypeStruct((NG, 2, widt...]
    all_gather x1 -> x0, waiting for transfers between devices: 38 us -> none  [all_blocks(): blocks = lax.all_gather(blocks, axes[k])]
    all_gather x2 -> x0, blocking collectives: 31.1 us -> none  [all_blocks(): blocks = lax.all_gather(blocks, axes[k])]
    all_to_all x1 -> x0, starting transfers between devices: 16 us -> none  [sent_to_all(): return lax.all_to_all(copies, axis, split_axis=0, concat_axis=0, tiled=True)]
    all_to_all x1 -> x0, waiting for transfers between devices: 9.34 us -> none  [sent_to_all(): return lax.all_to_all(copies, axis, split_axis=0, concat_axis=0, tiled=True)]
  transfers between devices with their start and end apart: 3 -> 0, of which waited for: 3 -> 0; matrix products, arithmetic and copies ran while one was open for 0% -> 0% of each run, Pallas kernels for 0% -> 0%
where the time goes in v2:
time: 96.7 us; the launch traced here: 96.4 us
  Pallas kernels  90.8 us (94%)
  local copies, waits for them, and re-layouts  3.52 us (4%)
  matrix products  2.11 us (2%)
    pallas_call x1, Pallas kernels, on_device(): pl.pallas_call(layer_kernel, out_shape=(jax.ShapeDtypeStruct((NG, 2, widt...  90.8 us
    dot_general x1, matrix products, on_device(): jnp.dot(owned.T, rows.reshape(NG * 2, width), preferred_element_type=f32)  2.11 us

profile of v2, /device:TPU:1, one launch (start us, length us, event | category | flops | bytes accessed | tf_op | source)
XLA Modules:
  0.0 96.4 jit_solution(2223873934103944472)
XLA Ops:
  0.0 1.3 %broadcast_in_dim.15.ids = s32[2,128]{1,0:T(2,128)} broadcast(s32[2]{0:T(128)} %bitcast.4), dimensions={0} | broadcast | bytes 1032 | tf_op jit(solution)/shard_map/broadcast_in_dim | solution.py:513
  1.3 1.3 %broadcast_in_dim.17.gates = f32[2,128]{1,0:T(2,128)} broadcast(f32[2]{0:T(128)} %bitcast.5), dimensions={0} | broadcast | bytes 1032 | tf_op jit(solution)/shard_map/broadcast_in_dim | solution.py:514
  2.6 90.8 %layer.1 = (bf16[8,2,4096]{2,1,0:T(2,128)(2,1)}, bf16[16,128]{1,0:T(8,128)(2,1)}) custom-call(s32[2,128]{1,0:T(2,128)} %broadcast_in_dim.15.ids, f32[2,128]{1,0:T(2,128)} %broadcast_in_dim.17.gates, bf16[192,192]{1,0:T(8,128)(2,1)} %constant.4.clone.perm, bf16[192,192]{1,0:T(8,128)(2,1)} %constant.5.clone.perm_t, bf16[128,4096]{1,0:T(8,128)(2,1)} %tokens_hbm.1, ...), custom_call_target="tpu_custom_call" | custom-call | tf_op jit(solution)/shard_map/layer/pallas_call | solution.py:499
  93.4 1.0 reshape.7
  94.3 2.1 %convolution_convert_fusion = bf16[128,4096]{1,0:T(8,128)(2,1)} fusion(bf16[16,128]{1,0:T(8,128)(2,1)} %get-tuple-element.7, bf16[16,4096]{1,0:T(8,128)(2,1)S(1)} %reshape.7), kind=kOutput, calls=%fused_computation | convolution fusion | flops 17301504 | bytes 1183744 | tf_op jit(solution)/shard_map/dot_general | solution.py:522

commit v3 on v2

--- a/solution.py
+++ b/solution.py
@@ -12,11 +12,12 @@
 NY, NZ, NX = 8, 3, 4
 NH, NC = 4, 2
 NG = NH * NC
-YC, XC = 3, 3
+YC, XC = 3, 6
 YR, XR = NX * NZ * 2 // YC, NY * NZ * 2 // XC
 ROWS = NX * NY * NZ * 2
 FAR_FIRST = [(h, c) for h in (2, 1, 3, 0) for c in range(NC) if h or c]
 LEFT, RIGHT = 0, 1
+LEFT_EIGHTHS = 3
 
 
 def remote(src, dst, send_sem, recv_sem, **where):
@@ -32,6 +33,10 @@
 
 def turn(index, by, size):
     return lax.rem(index + by + size, size)
+
+
+def far_first(size):
+    return sorted(range(1, size), key=lambda d: -min(d, size - d))
 
 
 def each(count):
@@ -110,25 +115,33 @@
 
 
 def layer_kernel(
-    ids,
-    gates,
-    perm,
-    perm_t,
+    ids_hbm,
+    gates_hbm,
+    perm_hbm,
+    perm_t_hbm,
     tokens_hbm,
     gate_hbm,
     up_hbm,
     down_hbm,
-    rows_out,
-    owned_out,
+    out_hbm,
+    ids_raw,
+    gates_raw,
+    perm,
+    perm_t,
+    ids,
+    gates,
     tokens,
     w_in,
     w_out,
     all_ids,
     owned,
     cand_f32,
-    cand,
-    arrived,
-    z_rows,
+    cand_l,
+    cand_r,
+    arrived_l,
+    arrived_r,
+    z_rows_l,
+    z_rows_r,
     x_rows,
     y_rows,
     flat_f32,
@@ -146,21 +159,31 @@
     mid_y_f32,
     mid_y,
     mid_y_got,
-    mid_z,
-    mid_z_got,
-    weighted,
-    gathered,
+    mid_z_l,
+    mid_z_r,
+    mid_z_got_l,
+    mid_z_got_r,
+    weighted_l,
+    weighted_r,
+    gathered_l,
+    gathered_r,
+    mixed,
     w_sem,
+    out_sem,
     *sems,
 ):
     y, z, x = lax.axis_index("y"), lax.axis_index("z"), lax.axis_index("x")
     g = lax.axis_index("grp")
     chip, core = g // NC, lax.rem(g, NC)
     tok_dev, width = tokens.shape
-    half = width // 2
     hid = gate_hbm.shape[1]
     pad = w_out.shape[0]
-    cols = (slice(0, half), slice(half, width))
+    wide = (x_rows.shape[-1], y_rows.shape[-1])
+    cols = (slice(0, wide[0]), slice(wide[0], width))
+    cand, arrived = (cand_l, cand_r), (arrived_l, arrived_r)
+    z_rows = (z_rows_l, z_rows_r)
+    mid_z, mid_z_got = (mid_z_l, mid_z_r), (mid_z_got_l, mid_z_got_r)
+    weighted, gathered = (weighted_l, weighted_r), (gathered_l, gathered_r)
     f32, bf16 = jnp.float32, jnp.bfloat16
     (
         (id_send, id_recv),
@@ -186,15 +209,23 @@
     def peer(h, c, sign=1):
         return turn(chip, sign * h, NH) * NC + turn(core, sign * c, NC)
 
+    small = [
+        pltpu.make_async_copy(src, dst, w_sem.at[n])
+        for n, (src, dst) in enumerate(((ids_hbm, ids_raw), (gates_hbm, gates_raw)))
+    ]
     loads = [
-        pltpu.make_async_copy(tokens_hbm, tokens, w_sem.at[0]),
-        pltpu.make_async_copy(gate_hbm.at[0], w_in.at[pl.ds(0, hid)], w_sem.at[1]),
-        pltpu.make_async_copy(up_hbm.at[0], w_in.at[pl.ds(pad, hid)], w_sem.at[2]),
-        pltpu.make_async_copy(down_hbm.at[0], w_out.at[pl.ds(0, hid)], w_sem.at[3]),
+        pltpu.make_async_copy(src, dst, w_sem.at[n + 2])
+        for n, (src, dst) in enumerate(
+            (
+                (tokens_hbm, tokens),
+                (perm_hbm, perm),
+                (perm_t_hbm, perm_t),
+                (gate_hbm.at[0], w_in.at[pl.ds(0, hid)]),
+                (up_hbm.at[0], w_in.at[pl.ds(pad, hid)]),
+                (down_hbm.at[0], w_out.at[pl.ds(0, hid)]),
+            )
+        )
     ]
-    for copy in loads:
-        copy.start()
-
     barrier = pltpu.get_barrier_semaphore()
     for h, c in FAR_FIRST:
         pl.semaphore_signal(barrier, device_id={"grp": peer(h, c)})
@@ -204,16 +235,23 @@
         pl.semaphore_signal(barrier, device_id={"x": turn(x, o, NX)})
     for o in range(1, NZ):
         pl.semaphore_signal(barrier, device_id={"z": turn(z, o, NZ)})
+    for copy in small + loads:
+        copy.start()
+    for at in (hid, pad + hid):
+        w_in[pl.ds(at, pad - hid), :] = jnp.zeros((pad - hid, width), bf16)
+    w_out[pl.ds(hid, pad - hid), :] = jnp.zeros((pad - hid, width), bf16)
+    for copy in small:
+        copy.wait()
+    for r in range(2):
+        ids[pl.ds(r, 1), :] = jnp.broadcast_to(ids_raw[:, r : r + 1], (1, tok_dev))
+        gates[pl.ds(r, 1), :] = jnp.broadcast_to(gates_raw[:, r : r + 1], (1, gates.shape[1]))
+    loads[0].wait()
     pl.semaphore_wait(barrier, NG + NZ + NX + NY - 4)
 
     for h, c in FAR_FIRST:
         at = h * NC + c
         go(remote(ids, all_ids.at[g], id_send.at[at], id_recv.at[at], grp=peer(h, c)))
     all_ids[g] = ids[...]
-    for at in (hid, pad + hid):
-        w_in[pl.ds(at, pad - hid), :] = jnp.zeros((pad - hid, width), bf16)
-    w_out[pl.ds(hid, pad - hid), :] = jnp.zeros((pad - hid, width), bf16)
-    loads[0].wait()
     for h, c in FAR_FIRST[::-1]:
         at, landed = h * NC + c, all_ids.at[peer(h, c, -1)]
         remote(landed, landed, id_send.at[at], id_recv.at[at], grp=peer(h, c)).wait_recv()
@@ -224,15 +262,15 @@
         owned[pl.ds(e * 2, 2), :] = (all_ids[e] == lane).astype(f32)
     chosen = owned[...].astype(bf16)
     for k in (RIGHT, LEFT):
-        cand_f32[...] = jnp.dot(chosen, tokens[:, cols[k]], preferred_element_type=f32)
+        cand_f32[:, : wide[k]] = jnp.dot(chosen, tokens[:, cols[k]], preferred_element_type=f32)
         for e in range(NG):
-            cand[k, e] = cand_f32[pl.ds(e * 2, 2), :].astype(bf16)
+            cand[k][e] = cand_f32[pl.ds(e * 2, 2), : wide[k]].astype(bf16)
         for h, c in FAR_FIRST:
             at, to = h * NC + c, peer(h, c)
             go(
                 remote(
-                    cand.at[k, to],
-                    arrived.at[k, at],
+                    cand[k].at[to],
+                    arrived[k].at[at],
                     row_send.at[k * NG + at],
                     row_recv.at[k * NG + at],
                     grp=to,
@@ -240,12 +278,12 @@
             )
 
     def spread(k, o):
-        src = z_rows.at[k, turn(z, -o, NZ)]
+        src = z_rows[k].at[turn(z, -o, NZ)]
         axis, me, size, buf, send, recv = (
             ("x", x, NX, x_rows, gx_send, gx_recv),
             ("y", y, NY, y_rows, gy_send, gy_recv),
         )[k]
-        for d in range(1, size):
+        for d in far_first(size):
             at = o * (size - 1) + d - 1
             dst = buf.at[me, turn(z, -o, NZ)]
             go(remote(src, dst, send.at[at], recv.at[at], **{axis: turn(me, d, size)}))
@@ -265,24 +303,24 @@
                 ).wait_recv()
 
     for k in (RIGHT, LEFT):
-        total = cand[k, g].astype(f32)
+        total = cand[k][g].astype(f32)
         for h, c in FAR_FIRST[::-1]:
             at = h * NC + c
-            landed = arrived.at[k, at]
+            landed = arrived[k].at[at]
             remote(
                 landed, landed, row_send.at[k * NG + at], row_recv.at[k * NG + at], grp=peer(h, c)
             ).wait_recv()
             total = total + landed[...].astype(f32)
-        z_rows[k, z] = total.astype(bf16)
+        z_rows[k][z] = total.astype(bf16)
         for o in range(1, NZ):
             at = k * (NZ - 1) + o - 1
-            ref = z_rows.at[k, z]
+            ref = z_rows[k].at[z]
             go(remote(ref, ref, gz_send.at[at], gz_recv.at[at], z=turn(z, o, NZ)))
         spread(k, 0)
     for k in (RIGHT, LEFT):
         for o in range(1, NZ):
             at = k * (NZ - 1) + o - 1
-            landed = z_rows.at[k, turn(z, -o, NZ)]
+            landed = z_rows[k].at[turn(z, -o, NZ)]
             remote(landed, landed, gz_send.at[at], gz_recv.at[at], z=turn(z, o, NZ)).wait_recv()
             spread(k, o)
 
@@ -292,9 +330,9 @@
     spread_wait(LEFT)
     for i in range(NX):
         for j in range(NZ):
-            flat_f32[pl.ds((i * NZ + j) * 2, 2), :] = x_rows[i, j].astype(f32)
+            flat_f32[pl.ds((i * NZ + j) * 2, 2), : wide[LEFT]] = x_rows[i, j].astype(f32)
     for c in range(YC):
-        ring_y[y * YC + c] = flat_f32[pl.ds(c * YR, YR), :].astype(bf16)
+        ring_y[y * YC + c] = flat_f32[pl.ds(c * YR, YR), : wide[LEFT]].astype(bf16)
     for c, way in each(YC):
         y_send(1, way, c)
     spread_wait(RIGHT)
@@ -308,11 +346,14 @@
     for c, way in each(YC):
         y_wait(1, way, c)
         y_send(2, way, c)
-    for c, way in each(YC):
-        y_wait(2, way, c)
-        y_send(3, way, c)
-        x_wait(1, way, c)
-        x_send(2, way, c)
+    for c in range(max(YC, XC)):
+        for way in range(2):
+            if c < YC:
+                y_wait(2, way, c)
+                y_send(3, way, c)
+            if c < XC:
+                x_wait(1, way, c)
+                x_send(2, way, c)
     for c, way in each(YC):
         y_wait(3, way, c)
         y_send(4, way, c)
@@ -322,7 +363,7 @@
         x_wait(2, way, c)
 
     def from_ring(ref, k):
-        rows = ref[...].astype(f32).reshape(ROWS, half).astype(bf16)
+        rows = ref[...].astype(f32).reshape(ROWS, wide[k]).astype(bf16)
         return lax.dot_general(
             rows, w_in[:, cols[k]], (((1,), (1,)), ((), ())), preferred_element_type=f32
         )
@@ -342,18 +383,21 @@
     y_first, y_add, y_last = ring_sum(go, "y", y, NY, YC, part_y, sum_y, got_y, *ring_sy)
     x_first, x_add, x_last = ring_sum(go, "x", x, NX, XC, part_x, sum_x, got_x, *ring_sx)
 
-    part_y[...] = jnp.dot(hidden, w_out[:, :half], preferred_element_type=f32).reshape(part_y.shape)
+    part_y[...] = jnp.dot(hidden, w_out[:, cols[LEFT]], preferred_element_type=f32).reshape(part_y.shape)
     for c in range(YC):
         y_first(c)
     hidden_t = jnp.dot(perm_t[...], hidden, preferred_element_type=f32).astype(bf16)
-    part_x[...] = jnp.dot(hidden_t, w_out[:, half:], preferred_element_type=f32).reshape(part_x.shape)
+    part_x[...] = jnp.dot(hidden_t, w_out[:, cols[RIGHT]], preferred_element_type=f32).reshape(part_x.shape)
     for c in range(XC):
         x_first(c)
     for c, way in each(YC):
         y_add(1, way, c)
-    for c, way in each(YC):
-        y_add(2, way, c)
-        x_add(1, way, c)
+    for c in range(max(YC, XC)):
+        for way in range(2):
+            if c < YC:
+                y_add(2, way, c)
+            if c < XC:
+                x_add(1, way, c)
     for c, way in each(YC):
         y_add(3, way, c)
 
@@ -363,23 +407,23 @@
     )
 
     def back(k, last, chunks, height):
-        axis, me, size, wide, buf, got, send, recv = mids[k]
+        axis, me, size, exact, buf, got, send, recv = mids[k]
         for c in range(chunks):
-            flat_f32[pl.ds(c * height, height), :] = last(c)
+            flat_f32[pl.ds(c * height, height), : wide[k]] = last(c)
         for i in range(size):
             for j in range(NZ):
-                rows = flat_f32[pl.ds((i * NZ + j) * 2, 2), :]
-                wide[i, j] = rows
+                rows = flat_f32[pl.ds((i * NZ + j) * 2, 2), : wide[k]]
+                exact[i, j] = rows
                 buf[i, j] = rows.astype(bf16)
         for o in (1, 2, 0):
-            for d in range(1, size):
+            for d in far_first(size):
                 at = o * (size - 1) + d - 1
                 src = buf.at[turn(me, d, size), turn(z, o, NZ)]
                 go(remote(src, got.at[at], send.at[at], recv.at[at], **{axis: turn(me, d, size)}))
 
     def back_sum(k, o):
-        axis, me, size, wide, buf, got, send, recv = mids[k]
-        total = wide[me, turn(z, o, NZ)]
+        axis, me, size, exact, buf, got, send, recv = mids[k]
+        total = exact[me, turn(z, o, NZ)]
         for d in range(1, size):
             at = o * (size - 1) + d - 1
             landed = got.at[at]
@@ -394,38 +438,52 @@
     for k in (LEFT, RIGHT):
         for o in range(1, NZ):
             at = k * (NZ - 1) + o - 1
-            mid_z[at] = back_sum(k, o).astype(bf16)
-            go(
-                remote(
-                    mid_z.at[at], mid_z_got.at[at], sz_send.at[at], sz_recv.at[at], z=turn(z, o, NZ)
-                )
-            )
+            ref, landed = mid_z[k].at[o - 1], mid_z_got[k].at[o - 1]
+            ref[...] = back_sum(k, o).astype(bf16)
+            go(remote(ref, landed, sz_send.at[at], sz_recv.at[at], z=turn(z, o, NZ)))
+    before = len(sent)
     for k in (LEFT, RIGHT):
         total = back_sum(k, 0)
         for o in range(1, NZ):
             at = k * (NZ - 1) + o - 1
-            landed = mid_z_got.at[at]
+            landed = mid_z_got[k].at[o - 1]
             remote(landed, landed, sz_send.at[at], sz_recv.at[at], z=turn(z, o, NZ)).wait_recv()
             total = total + landed[...].astype(f32)
-        weighted[k] = (gates[:, :1] * total.astype(bf16).astype(f32)).astype(bf16)
+        weighted[k][...] = (gates[:, :1] * total.astype(bf16).astype(f32)).astype(bf16)
         for h, c in FAR_FIRST:
             at = k * NG + h * NC + c
             go(
                 remote(
-                    weighted.at[k], gathered.at[k, g], out_send.at[at], out_recv.at[at], grp=peer(h, c)
+                    weighted[k],
+                    gathered[k].at[g],
+                    out_send.at[at],
+                    out_recv.at[at],
+                    grp=peer(h, c),
                 )
             )
-        gathered[k, g] = weighted[k]
-
-    owned_out[...] = chosen
+        gathered[k][g] = weighted[k][...]
+
+    for copy in sent[:before]:
+        copy.wait_send()
+    chosen_t = owned[...].T.astype(bf16)
+    stores = []
     for k in (LEFT, RIGHT):
         for h, c in FAR_FIRST[::-1]:
             at = k * NG + h * NC + c
-            landed = gathered.at[k, peer(h, c, -1)]
+            landed = gathered[k].at[peer(h, c, -1)]
             remote(landed, landed, out_send.at[at], out_recv.at[at], grp=peer(h, c)).wait_recv()
-        rows_out[:, :, cols[k]] = gathered[k]
-    for copy in sent:
+        for e in range(NG):
+            cand_f32[pl.ds(e * 2, 2), : wide[k]] = gathered[k][e].astype(f32)
+        rows = cand_f32[:, : wide[k]].astype(bf16)
+        mixed[:, cols[k]] = jnp.dot(chosen_t, rows, preferred_element_type=f32).astype(bf16)
+        stores.append(
+            pltpu.make_async_copy(mixed.at[:, cols[k]], out_hbm.at[:, cols[k]], out_sem.at[k])
+        )
+        stores[-1].start()
+    for copy in sent[before:]:
         copy.wait_send()
+    for copy in stores:
+        copy.wait()
 
 
 def swap_matrix():
@@ -439,43 +497,60 @@
 
 def on_device(tokens, select, gates, gate_proj, up_proj, down_proj):
     tok_dev, width = tokens.shape
-    half = width // 2
+    left = width * LEFT_EIGHTHS // 8
+    right = width - left
+    most = max(left, right)
     bf16, f32 = jnp.bfloat16, jnp.float32
     dma, vmem = pltpu.SemaphoreType.DMA, pltpu.VMEM
     hops_y, hops_x = NY * YC, NX * XC
     pad = -(-gate_proj.shape[1] // 128) * 128
     scratch = [
+        vmem((1, 2), jnp.int32),
+        vmem((1, 2), f32),
+        vmem((ROWS, ROWS), bf16),
+        vmem((ROWS, ROWS), bf16),
+        vmem((2, tok_dev), jnp.int32),
+        vmem((2, 128), f32),
         vmem((tok_dev, width), bf16),
         vmem((2 * pad, width), bf16),
         vmem((pad, width), bf16),
         vmem((NG, 2, tok_dev), jnp.int32),
         vmem((NG * 2, tok_dev), f32),
-        vmem((NG * 2, half), f32),
-        vmem((2, NG, 2, half), bf16),
-        vmem((2, NG, 2, half), bf16),
-        vmem((2, NZ, 2, half), bf16),
-        vmem((NX, NZ, 2, half), bf16),
-        vmem((NY, NZ, 2, half), bf16),
-        vmem((NY * NZ * 2, half), f32),
-        vmem((NY * YC, YR, half), bf16),
-        vmem((NX * XC, XR, half), bf16),
-        vmem((NY * YC, YR, half), f32),
-        vmem((NX * XC, XR, half), f32),
-        vmem((NY * YC, YR, half), bf16),
-        vmem((NX * XC, XR, half), bf16),
-        vmem((hops_y, YR, half), bf16),
-        vmem((hops_x, XR, half), bf16),
-        vmem((NX, NZ, 2, half), f32),
-        vmem((NX, NZ, 2, half), bf16),
-        vmem((NZ * (NX - 1), 2, half), bf16),
-        vmem((NY, NZ, 2, half), f32),
-        vmem((NY, NZ, 2, half), bf16),
-        vmem((NZ * (NY - 1), 2, half), bf16),
-        vmem((2 * (NZ - 1), 2, half), bf16),
-        vmem((2 * (NZ - 1), 2, half), bf16),
-        vmem((2, 2, half), bf16),
-        vmem((2, NG, 2, half), bf16),
-        dma((4,)),
+        vmem((NG * 2, most), f32),
+        vmem((NG, 2, left), bf16),
+        vmem((NG, 2, right), bf16),
+        vmem((NG, 2, left), bf16),
+        vmem((NG, 2, right), bf16),
+        vmem((NZ, 2, left), bf16),
+        vmem((NZ, 2, right), bf16),
+        vmem((NX, NZ, 2, left), bf16),
+        vmem((NY, NZ, 2, right), bf16),
+        vmem((NY * NZ * 2, most), f32),
+        vmem((NY * YC, YR, left), bf16),
+        vmem((NX * XC, XR, right), bf16),
+        vmem((NY * YC, YR, left), f32),
+        vmem((NX * XC, XR, right), f32),
+        vmem((NY * YC, YR, left), bf16),
+        vmem((NX * XC, XR, right), bf16),
+        vmem((hops_y, YR, left), bf16),
+        vmem((hops_x, XR, right), bf16),
+        vmem((NX, NZ, 2, left), f32),
+        vmem((NX, NZ, 2, left), bf16),
+        vmem((NZ * (NX - 1), 2, left), bf16),
+        vmem((NY, NZ, 2, right), f32),
+        vmem((NY, NZ, 2, right), bf16),
+        vmem((NZ * (NY - 1), 2, right), bf16),
+        vmem((NZ - 1, 2, left), bf16),
+        vmem((NZ - 1, 2, right), bf16),
+        vmem((NZ - 1, 2, left), bf16),
+        vmem((NZ - 1, 2, right), bf16),
+        vmem((2, left), bf16),
+        vmem((2, right), bf16),
+        vmem((NG, 2, left), bf16),
+        vmem((NG, 2, right), bf16),
+        vmem((tok_dev, width), bf16),
+        dma((8,)),
+        dma((2,)),
     ]
     for count in (
         NG,
@@ -493,25 +568,21 @@
         2 * NG,
     ):
         scratch += [dma((count,)), dma((count,))]
-    in_vmem = pl.BlockSpec(memory_space=pltpu.VMEM)
     in_hbm = pl.BlockSpec(memory_space=pl.ANY)
     table = swap_matrix()
-    rows, owned = pl.pallas_call(
+    return pl.pallas_call(
         layer_kernel,
-        out_shape=(
-            jax.ShapeDtypeStruct((NG, 2, width), bf16),
-            jax.ShapeDtypeStruct((NG * 2, tok_dev), bf16),
-        ),
-        in_specs=[in_vmem] * 4 + [in_hbm] * 4,
-        out_specs=(in_vmem, in_vmem),
+        out_shape=jax.ShapeDtypeStruct((tok_dev, width), bf16),
+        in_specs=[in_hbm] * 8,
+        out_specs=in_hbm,
         scratch_shapes=scratch,
         compiler_params=pltpu.CompilerParams(
             collective_id=0, has_side_effects=True, vmem_limit_bytes=56 * 1024 * 1024
         ),
         name="layer",
     )(
-        jnp.broadcast_to(select.reshape(2, 1), (2, tok_dev)),
-        jnp.broadcast_to(gates.reshape(2, 1), (2, 128)),
+        select,
+        gates,
         jnp.asarray(table, bf16),
         jnp.asarray(table.T, bf16),
         tokens,
@@ -519,8 +590,6 @@
         up_proj,
         down_proj,
     )
-    mixed = jnp.dot(owned.T, rows.reshape(NG * 2, width), preferred_element_type=f32)
-    return mixed.astype(bf16)
 
 
 def solution(mesh):

time: 96.7 us -> 91.8 us (0.949)
  matrix products: 2.11 us -> 0 us
  Pallas kernels: 90.8 us -> 89.3 us
  local copies, waits for them, and re-layouts: 3.52 us -> 2.29 us
    broadcast_in_dim x2 -> x0, local copies, waits for them, and re-layouts: 2.57 us -> none  [the longest x1 1.28 us: on_device(): jnp.broadcast_to(select.reshape(2, 1), (2, tok_dev))]
    unnamed x0 -> x1, local copies, waits for them, and re-layouts: none -> 2.29 us
    dot_general x1 -> x0, matrix products: 2.11 us -> none  [on_device(): jnp.dot(owned.T, rows.reshape(NG * 2, width), preferred_element_type=f32)]
    pallas_call x1, Pallas kernels: 90.8 us -> 89.3 us  [on_device(): pl.pallas_call(layer_kernel, out_shape=jax.ShapeDtypeStruct((tok_dev, wid...]
where the time goes in v3:
time: 91.8 us; the launch traced here: 91.6 us
  Pallas kernels  89.3 us (97%)
  local copies, waits for them, and re-layouts  2.29 us (2%)
    pallas_call x1, Pallas kernels, on_device(): pl.pallas_call(layer_kernel, out_shape=jax.ShapeDtypeStruct((tok_dev, wid...  89.3 us
    unnamed x1, local copies, waits for them, and re-layouts  2.29 us

profile of v3, /device:TPU:1, one launch (start us, length us, event | category | flops | bytes accessed | tf_op | source)
XLA Modules:
  0.0 91.6 jit_solution(6793961469146053549)
XLA Ops:
  0.0 89.3 %layer.1 = bf16[128,4096]{1,0:T(8,128)(2,1)} custom-call(s32[1,2]{1,0:T(1,128)} %ids_hbm.1, f32[1,2]{1,0:T(1,128)} %gates_hbm.1, bf16[192,192]{1,0:T(8,128)(2,1)} %constant.4.clone.perm_hbm, bf16[192,192]{1,0:T(8,128)(2,1)} %constant.5.clone.perm_t_hbm, bf16[128,4096]{1,0:T(8,128)(2,1)} %tokens_hbm.1, bf16[1,112,4096]{2,1,0:T(8,128)(2,1)} %gate_hbm.1, ...), custom_call_target="tpu_custom_call" | custom-call | tf_op jit(solution)/shard_map/layer/pallas_call | solution.py:573
  89.3 2.3 %copy.10 = bf16[128,4096]{1,0:T(8,128)(2,1)} copy(bf16[128,4096]{1,0:T(8,128)(2,1)} %layer.1) | data formatting | bytes 2097152

commit v4 on v3

--- a/solution.py
+++ b/solution.py
@@ -16,6 +16,7 @@
 YR, XR = NX * NZ * 2 // YC, NY * NZ * 2 // XC
 ROWS = NX * NY * NZ * 2
 FAR_FIRST = [(h, c) for h in (2, 1, 3, 0) for c in range(NC) if h or c]
+CHIPS = (2, 1, 3)
 LEFT, RIGHT = 0, 1
 LEFT_EIGHTHS = 3
 
@@ -86,9 +87,8 @@
             **{axis: turn(me, sign, size)},
         )
 
-    def first(c):
-        at = turn(me, steps, size) * chunks + c
-        buf[at] = parts[at].astype(bf16)
+    def first(c, rows):
+        buf[turn(me, steps, size) * chunks + c] = rows.astype(bf16)
         for way in range(2):
             go(copy(1, way, c))
 
@@ -123,7 +123,7 @@
     gate_hbm,
     up_hbm,
     down_hbm,
-    out_hbm,
+    mixed,
     ids_raw,
     gates_raw,
     perm,
@@ -138,6 +138,10 @@
     cand_f32,
     cand_l,
     cand_r,
+    pair_l,
+    pair_r,
+    merged_l,
+    merged_r,
     arrived_l,
     arrived_r,
     z_rows_l,
@@ -147,6 +151,8 @@
     flat_f32,
     ring_y,
     ring_x,
+    hid_y,
+    hid_x,
     part_y,
     part_x,
     sum_y,
@@ -167,9 +173,7 @@
     weighted_r,
     gathered_l,
     gathered_r,
-    mixed,
     w_sem,
-    out_sem,
     *sems,
 ):
     y, z, x = lax.axis_index("y"), lax.axis_index("z"), lax.axis_index("x")
@@ -181,6 +185,7 @@
     wide = (x_rows.shape[-1], y_rows.shape[-1])
     cols = (slice(0, wide[0]), slice(wide[0], width))
     cand, arrived = (cand_l, cand_r), (arrived_l, arrived_r)
+    pair, merged = (pair_l, pair_r), (merged_l, merged_r)
     z_rows = (z_rows_l, z_rows_r)
     mid_z, mid_z_got = (mid_z_l, mid_z_r), (mid_z_got_l, mid_z_got_r)
     weighted, gathered = (weighted_l, weighted_r), (gathered_l, gathered_r)
@@ -264,16 +269,30 @@
     for k in (RIGHT, LEFT):
         cand_f32[:, : wide[k]] = jnp.dot(chosen, tokens[:, cols[k]], preferred_element_type=f32)
         for e in range(NG):
-            cand[k][e] = cand_f32[pl.ds(e * 2, 2), : wide[k]].astype(bf16)
-        for h, c in FAR_FIRST:
-            at, to = h * NC + c, peer(h, c)
+            cand[k][e % NC, e // NC] = cand_f32[pl.ds(e * 2, 2), : wide[k]].astype(bf16)
+        go(
+            remote(
+                cand[k].at[1 - core],
+                pair[k],
+                row_send.at[k * NH],
+                row_recv.at[k * NH],
+                grp=peer(0, 1),
+            )
+        )
+    for k in (RIGHT, LEFT):
+        remote(
+            pair[k], pair[k], row_send.at[k * NH], row_recv.at[k * NH], grp=peer(0, 1)
+        ).wait_recv()
+        merged[k][...] = (cand[k][core].astype(f32) + pair[k][...].astype(f32)).astype(bf16)
+        for h in CHIPS:
+            at = k * NH + h
             go(
                 remote(
-                    cand[k].at[to],
-                    arrived[k].at[at],
-                    row_send.at[k * NG + at],
-                    row_recv.at[k * NG + at],
-                    grp=to,
+                    merged[k].at[turn(chip, h, NH)],
+                    arrived[k].at[h - 1],
+                    row_send.at[at],
+                    row_recv.at[at],
+                    grp=peer(h, 0),
                 )
             )
 
@@ -303,12 +322,11 @@
                 ).wait_recv()
 
     for k in (RIGHT, LEFT):
-        total = cand[k][g].astype(f32)
-        for h, c in FAR_FIRST[::-1]:
-            at = h * NC + c
-            landed = arrived[k].at[at]
+        total = merged[k][chip].astype(f32)
+        for h in CHIPS[::-1]:
+            at, landed = k * NH + h, arrived[k].at[h - 1]
             remote(
-                landed, landed, row_send.at[k * NG + at], row_recv.at[k * NG + at], grp=peer(h, c)
+                landed, landed, row_send.at[at], row_recv.at[at], grp=peer(h, 0)
             ).wait_recv()
             total = total + landed[...].astype(f32)
         z_rows[k][z] = total.astype(bf16)
@@ -378,18 +396,26 @@
         y_wait(4, way, c)
     act = act + from_ring(ring_y, LEFT)
     gate_act, up_act = act[:, :pad], act[:, pad:]
-    hidden = (gate_act / (1.0 + jnp.exp(-gate_act)) * up_act).astype(bf16)
+    hidden = gate_act / (1.0 + jnp.exp(-gate_act)) * up_act
+    hid_y[...] = hidden.reshape(hid_y.shape).astype(bf16)
+    hidden = hidden.astype(bf16)
 
     y_first, y_add, y_last = ring_sum(go, "y", y, NY, YC, part_y, sum_y, got_y, *ring_sy)
     x_first, x_add, x_last = ring_sum(go, "x", x, NX, XC, part_x, sum_x, got_x, *ring_sx)
 
-    part_y[...] = jnp.dot(hidden, w_out[:, cols[LEFT]], preferred_element_type=f32).reshape(part_y.shape)
+    def down(rows, k):
+        return jnp.dot(rows, w_out[:, cols[k]], preferred_element_type=f32)
+
+    far = down(hid_y[turn(y, NY // 2, NY)], LEFT)
     for c in range(YC):
-        y_first(c)
-    hidden_t = jnp.dot(perm_t[...], hidden, preferred_element_type=f32).astype(bf16)
-    part_x[...] = jnp.dot(hidden_t, w_out[:, cols[RIGHT]], preferred_element_type=f32).reshape(part_x.shape)
+        y_first(c, far[c * YR : (c + 1) * YR])
+    hidden_t = jnp.dot(perm_t[...], hidden, preferred_element_type=f32)
+    hid_x[...] = hidden_t.reshape(hid_x.shape).astype(bf16)
+    far = down(hid_x[turn(x, NX // 2, NX)], RIGHT)
     for c in range(XC):
-        x_first(c)
+        x_first(c, far[c * XR : (c + 1) * XR])
+    part_y[...] = down(hidden, LEFT).reshape(part_y.shape)
+    part_x[...] = down(hidden_t.astype(bf16), RIGHT).reshape(part_x.shape)
     for c, way in each(YC):
         y_add(1, way, c)
     for c in range(max(YC, XC)):
@@ -450,40 +476,41 @@
             remote(landed, landed, sz_send.at[at], sz_recv.at[at], z=turn(z, o, NZ)).wait_recv()
             total = total + landed[...].astype(f32)
         weighted[k][...] = (gates[:, :1] * total.astype(bf16).astype(f32)).astype(bf16)
-        for h, c in FAR_FIRST:
-            at = k * NG + h * NC + c
+        gathered[k][core, chip] = weighted[k][...]
+        for h in CHIPS + (0,):
+            at = k * 2 * NH + h
             go(
                 remote(
                     weighted[k],
-                    gathered[k].at[g],
+                    gathered[k].at[core, chip],
                     out_send.at[at],
                     out_recv.at[at],
-                    grp=peer(h, c),
+                    grp=peer(h, 0) if h else peer(0, 1),
                 )
             )
-        gathered[k][g] = weighted[k][...]
 
     for copy in sent[:before]:
         copy.wait_send()
     chosen_t = owned[...].T.astype(bf16)
-    stores = []
+
+    def landing(k, side, h):
+        return gathered[k].at[side, turn(chip, -h, NH)]
+
     for k in (LEFT, RIGHT):
-        for h, c in FAR_FIRST[::-1]:
-            at = k * NG + h * NC + c
-            landed = gathered[k].at[peer(h, c, -1)]
-            remote(landed, landed, out_send.at[at], out_recv.at[at], grp=peer(h, c)).wait_recv()
+        for h in CHIPS[::-1]:
+            at, ref = k * 2 * NH + h, landing(k, core, h)
+            remote(ref, ref, out_send.at[at], out_recv.at[at], grp=peer(h, 0)).wait_recv()
+            go(remote(ref, ref, out_send.at[at + NH], out_recv.at[at + NH], grp=peer(0, 1)))
+    for k in (LEFT, RIGHT):
+        for h in (0,) + CHIPS[::-1]:
+            at, ref = k * 2 * NH + h + (NH if h else 0), landing(k, 1 - core, h)
+            remote(ref, ref, out_send.at[at], out_recv.at[at], grp=peer(0, 1)).wait_recv()
         for e in range(NG):
-            cand_f32[pl.ds(e * 2, 2), : wide[k]] = gathered[k][e].astype(f32)
+            cand_f32[pl.ds(e * 2, 2), : wide[k]] = gathered[k][e % NC, e // NC].astype(f32)
         rows = cand_f32[:, : wide[k]].astype(bf16)
         mixed[:, cols[k]] = jnp.dot(chosen_t, rows, preferred_element_type=f32).astype(bf16)
-        stores.append(
-            pltpu.make_async_copy(mixed.at[:, cols[k]], out_hbm.at[:, cols[k]], out_sem.at[k])
-        )
-        stores[-1].start()
     for copy in sent[before:]:
         copy.wait_send()
-    for copy in stores:
-        copy.wait()
 
 
 def swap_matrix():
@@ -517,10 +544,14 @@
         vmem((NG, 2, tok_dev), jnp.int32),
         vmem((NG * 2, tok_dev), f32),
         vmem((NG * 2, most), f32),
-        vmem((NG, 2, left), bf16),
-        vmem((NG, 2, right), bf16),
-        vmem((NG, 2, left), bf16),
-        vmem((NG, 2, right), bf16),
+        vmem((NC, NH, 2, left), bf16),
+        vmem((NC, NH, 2, right), bf16),
+        vmem((NH, 2, left), bf16),
+        vmem((NH, 2, right), bf16),
+        vmem((NH, 2, left), bf16),
+        vmem((NH, 2, right), bf16),
+        vmem((NH - 1, 2, left), bf16),
+        vmem((NH - 1, 2, right), bf16),
         vmem((NZ, 2, left), bf16),
         vmem((NZ, 2, right), bf16),
         vmem((NX, NZ, 2, left), bf16),
@@ -528,6 +559,8 @@
         vmem((NY * NZ * 2, most), f32),
         vmem((NY * YC, YR, left), bf16),
         vmem((NX * XC, XR, right), bf16),
+        vmem((NY, YC * YR, pad), bf16),
+        vmem((NX, XC * XR, pad), bf16),
         vmem((NY * YC, YR, left), f32),
         vmem((NX * XC, XR, right), f32),
         vmem((NY * YC, YR, left), bf16),
@@ -546,15 +579,13 @@
         vmem((NZ - 1, 2, right), bf16),
         vmem((2, left), bf16),
         vmem((2, right), bf16),
-        vmem((NG, 2, left), bf16),
-        vmem((NG, 2, right), bf16),
-        vmem((tok_dev, width), bf16),
+        vmem((NC, NH, 2, left), bf16),
+        vmem((NC, NH, 2, right), bf16),
         dma((8,)),
-        dma((2,)),
     ]
     for count in (
         NG,
-        2 * NG,
+        2 * NH,
         2 * (NZ - 1),
         NZ * (NX - 1),
         NZ * (NY - 1),
@@ -565,22 +596,12 @@
         NZ * (NX - 1),
         NZ * (NY - 1),
         2 * (NZ - 1),
-        2 * NG,
+        4 * NH,
     ):
         scratch += [dma((count,)), dma((count,))]
-    in_hbm = pl.BlockSpec(memory_space=pl.ANY)
+    in_hbm = pl.BlockSpec(memory_space=pltpu.HBM)
     table = swap_matrix()
-    return pl.pallas_call(
-        layer_kernel,
-        out_shape=jax.ShapeDtypeStruct((tok_dev, width), bf16),
-        in_specs=[in_hbm] * 8,
-        out_specs=in_hbm,
-        scratch_shapes=scratch,
-        compiler_params=pltpu.CompilerParams(
-            collective_id=0, has_side_effects=True, vmem_limit_bytes=56 * 1024 * 1024
-        ),
-        name="layer",
-    )(
+    arrays = (
         select,
         gates,
         jnp.asarray(table, bf16),
@@ -590,6 +611,17 @@
         up_proj,
         down_proj,
     )
+    return pl.pallas_call(
+        layer_kernel,
+        out_shape=jax.ShapeDtypeStruct((tok_dev, width), bf16),
+        in_specs=[in_hbm] * 8,
+        out_specs=pl.BlockSpec(memory_space=pltpu.VMEM),
+        scratch_shapes=scratch,
+        compiler_params=pltpu.CompilerParams(
+            collective_id=0, has_side_effects=True, vmem_limit_bytes=28 * 1024 * 1024
+        ),
+        name="layer",
+    )(*(pltpu.with_memory_space_constraint(a, pltpu.HBM) for a in arrays))
 
 
 def solution(mesh):

time: 91.8 us -> 88.9 us (0.968)
  Pallas kernels: 89.3 us -> 87.8 us
  local copies, waits for them, and re-layouts: 2.29 us -> 0.97 us
    pallas_call x1, Pallas kernels: 89.3 us -> 87.8 us  [on_device(): pl.pallas_call(layer_kernel, out_shape=jax.ShapeDtypeStruct((tok_dev, wid...]
    unnamed x1, local copies, waits for them, and re-layouts: 2.29 us -> 0.97 us
where the time goes in v4:
time: 88.9 us; the launch traced here: 88.8 us
  Pallas kernels  87.8 us (99%)
  local copies, waits for them, and re-layouts  0.97 us (1%)
    pallas_call x1, Pallas kernels, on_device(): pl.pallas_call(layer_kernel, out_shape=jax.ShapeDtypeStruct((tok_dev, wid...  87.8 us

profile of v4, /device:TPU:1, one launch (start us, length us, event | category | flops | bytes accessed | tf_op | source)
XLA Modules:
  0.0 88.8 jit_solution(1126655686042272846)
XLA Ops:
  0.0 87.8 %layer.1 = bf16[128,4096]{1,0:T(8,128)(2,1)S(1)} custom-call(s32[1,2]{1,0:T(1,128)} %ids_hbm.1, f32[1,2]{1,0:T(1,128)} %gates_hbm.1, bf16[192,192]{1,0:T(8,128)(2,1)} %constant.4.clone.perm_hbm, bf16[192,192]{1,0:T(8,128)(2,1)} %constant.5.clone.perm_t_hbm, bf16[128,4096]{1,0:T(8,128)(2,1)} %tokens_hbm.1, bf16[1,112,4096]{2,1,0:T(8,128)(2,1)} %gate_hbm.1, ...), custom_call_target="tpu_custom_call" | custom-call | tf_op jit(solution)/shard_map/layer/pallas_call | solution.py:614
  87.8 1.0 %copy.10 = bf16[128,4096]{1,0:T(8,128)(2,1)} copy(bf16[128,4096]{1,0:T(8,128)(2,1)S(1)} %layer.1) | data formatting | bytes 2097152

commit v5 on v4

--- a/solution.py
+++ b/solution.py
@@ -346,21 +346,19 @@
     x_send, x_wait = ring_gather(go, "x", x, NX, XC, ring_x, *ring_gx)
 
     spread_wait(LEFT)
-    for i in range(NX):
-        for j in range(NZ):
-            flat_f32[pl.ds((i * NZ + j) * 2, 2), : wide[LEFT]] = x_rows[i, j].astype(f32)
     for c in range(YC):
+        for p in range(c * YR // 2, (c + 1) * YR // 2):
+            flat_f32[pl.ds(p * 2, 2), : wide[LEFT]] = x_rows[p // NZ, p % NZ].astype(f32)
         ring_y[y * YC + c] = flat_f32[pl.ds(c * YR, YR), : wide[LEFT]].astype(bf16)
-    for c, way in each(YC):
-        y_send(1, way, c)
+        for way in range(2):
+            y_send(1, way, c)
     spread_wait(RIGHT)
-    for i in range(NY):
-        for j in range(NZ):
-            flat_f32[pl.ds((i * NZ + j) * 2, 2), :] = y_rows[i, j].astype(f32)
     for c in range(XC):
-        ring_x[x * XC + c] = flat_f32[pl.ds(c * XR, XR), :].astype(bf16)
-    for c, way in each(XC):
-        x_send(1, way, c)
+        for p in range(c * XR // 2, (c + 1) * XR // 2):
+            flat_f32[pl.ds(p * 2, 2), : wide[RIGHT]] = y_rows[p // NZ, p % NZ].astype(f32)
+        ring_x[x * XC + c] = flat_f32[pl.ds(c * XR, XR), : wide[RIGHT]].astype(bf16)
+        for way in range(2):
+            x_send(1, way, c)
     for c, way in each(YC):
         y_wait(1, way, c)
         y_send(2, way, c)
@@ -436,9 +434,9 @@
         axis, me, size, exact, buf, got, send, recv = mids[k]
         for c in range(chunks):
             flat_f32[pl.ds(c * height, height), : wide[k]] = last(c)
-        for i in range(size):
-            for j in range(NZ):
-                rows = flat_f32[pl.ds((i * NZ + j) * 2, 2), : wide[k]]
+            for first in range(c * height, (c + 1) * height, 2):
+                rows = flat_f32[pl.ds(first, 2), : wide[k]]
+                i, j = first // 2 // NZ, first // 2 % NZ
                 exact[i, j] = rows
                 buf[i, j] = rows.astype(bf16)
         for o in (1, 2, 0):

time: 88.9 us -> 88.7 us (level)
  no operation moved by 1% of the time
where the time goes in v5:
time: 88.7 us; the launch traced here: 88.6 us
  Pallas kernels  87.6 us (99%)
  local copies, waits for them, and re-layouts  0.97 us (1%)
    pallas_call x1, Pallas kernels, on_device(): pl.pallas_call(layer_kernel, out_shape=jax.ShapeDtypeStruct((tok_dev, wid...  87.6 us

profile of v5, /device:TPU:1, one launch (start us, length us, event | category | flops | bytes accessed | tf_op | source)
XLA Modules:
  0.0 88.6 jit_solution(15915664834140255695)
XLA Ops:
  0.0 87.6 %layer.1 = bf16[128,4096]{1,0:T(8,128)(2,1)S(1)} custom-call(s32[1,2]{1,0:T(1,128)} %ids_hbm.1, f32[1,2]{1,0:T(1,128)} %gates_hbm.1, bf16[192,192]{1,0:T(8,128)(2,1)} %constant.4.clone.perm_hbm, bf16[192,192]{1,0:T(8,128)(2,1)} %constant.5.clone.perm_t_hbm, bf16[128,4096]{1,0:T(8,128)(2,1)} %tokens_hbm.1, bf16[1,112,4096]{2,1,0:T(8,128)(2,1)} %gate_hbm.1, ...), custom_call_target="tpu_custom_call" | custom-call | tf_op jit(solution)/shard_map/layer/pallas_call | solution.py:612
  87.6 1.0 %copy.10 = bf16[128,4096]{1,0:T(8,128)(2,1)} copy(bf16[128,4096]{1,0:T(8,128)(2,1)S(1)} %layer.1) | data formatting | bytes 2097152
